TPU v7x, 32 devices: a whole 2x2x4 slice. The times are simulated.
32 devices in a mesh: tile: 8 (over z, x), dir: 4 (over y, core).
Axes of the slice: x: 2, y: 2, z: 4, core: 2. Of those that a mesh axis runs over, the one named last changes fastest.
Arguments:
- layers: bfloat16 [4, 1024, 2048], P('dir', 'tile'), may hold values from -6 to 6
- offsets: int32 [4, 4, 2], replicated, may hold values from 0 to 8191, as said below
- subap_valid: int32 [8, 16], P('tile'), may hold values from 0 to 1, as said below
- defocus: float32 [3], replicated, may hold values from -0.08 to 0.08
- weights: float32 [3], replicated, may hold values from 0.25 to 1
Outputs:
- spots: bfloat16 [4, 8, 128, 2048], P('dir', 'tile')
Inputs may be any that keep to these rules, and one draw needn't show every extreme that they name: offsets[d, l, 0] < 1024 and offsets[d, l, 1] < 8192; both bounds minus one are taken by some pair in every draw. `subap_valid`: the part of an annulus of lit subapertures that falls in the strip, with a few dead ones.
All inputs are finite; a program needn't handle non-finite values.
Results may differ from a plain program's by a relative error of at most 0.0055.
Values may be sent and summed in bfloat16 or wider, within the bound.
A program may use at most 64 MiB of HBM per device.

v0:
```python
import functools
import math

import jax
import jax.numpy as jnp
import numpy as np
from jax import lax
from jax.experimental import pallas as pl
from jax.experimental.pallas import tpu as pltpu
from jax.sharding import PartitionSpec as P

OVER = 2
QUANT = 4
REACH = 2
LANES = 128
CHUNKS = 8
MESH = pl.DeviceIdType.MESH
HALF_PI_HI = 1.5703125
HALF_PI_LO = math.pi / 2 - 1.5703125


def base_tables(n):
    frequency = np.arange(n, dtype=np.float64) - n // 2
    position = np.arange(n, dtype=np.float64) - (n - 1) / 2.0
    angle = -2.0 * math.pi / (OVER * n) * frequency[:, None] * position[None, :]
    factor = 1.0 / math.sqrt(n)
    return (np.cos(angle) * factor).astype(np.float32), (np.sin(angle) * factor).astype(np.float32)


def cos_sin(angle):
    turns = jnp.round(angle * (2.0 / math.pi))
    rest = (angle - turns * HALF_PI_HI) - turns * HALF_PI_LO
    quadrant = turns.astype(jnp.int32)
    square = rest * rest
    sin = rest + rest * square * (-1.0 / 6 + square * (1.0 / 120 - square * (1.0 / 5040)))
    cos = 1.0 + square * (-0.5 + square * (1.0 / 24 - square * (1.0 / 720 - square * (1.0 / 40320))))
    swap = (quadrant & 1) == 1
    cos_value = jnp.where(swap, sin, cos)
    sin_value = jnp.where(swap, cos, sin)
    cos_value = jnp.where(((quadrant + 1) & 2) == 2, -cos_value, cos_value)
    sin_value = jnp.where((quadrant & 2) == 2, -sin_value, sin_value)
    return cos_value, sin_value


def kernel(
    tiles, n, blocks, slices,
    x_ref, off_ref, valid_ref, defocus_ref, weights_ref, fr_ref, fi_ref, right_ref,
    out_ref,
    ext, shifted, mix, slide, send_buf, recv_buf, local, left, col_cos, col_sin,
    z_send, z_recv, s_send, s_recv, o_send, o_recv, p_send, p_recv, y_send, y_recv,
):
    tile = lax.axis_index("tile")
    own = lax.axis_index("dir")
    core = lax.rem(own, 2)
    chip = lax.div(own, 2)
    other_core = chip * 2 + (1 - core)
    other_chip = (1 - chip) * 2 + core
    odd = lax.rem(tile, 2)
    mate = tile + 1 - 2 * odd
    below = lax.rem(tile + tiles - 2, tiles)
    above = lax.rem(tile + 2, tiles)

    barrier = pltpu.get_barrier_semaphore()
    for device in ((tile, other_core), (tile, other_chip), (mate, own), (below, own), (above, own)):
        pl.semaphore_signal(barrier, inc=1, device_id=device, device_id_type=MESH)
    pl.semaphore_wait(barrier, 5)

    rows = n // CHUNKS
    pairs = blocks // 2

    def copy(source, target, send, recv, device):
        return pltpu.make_async_remote_copy(
            src_ref=source, dst_ref=target, send_sem=send, recv_sem=recv,
            device_id=device, device_id_type=MESH,
        )

    def z_copy(k):
        return copy(
            x_ref.at[0, pl.ds(k * rows, rows)], ext.at[core, 2, pl.ds(k * rows, rows)],
            z_send.at[k], z_recv.at[k], (below, own),
        )

    def first_copy(k):
        return copy(
            x_ref.at[0, pl.ds(k * rows, rows)], ext.at[core, 1, pl.ds(k * rows, rows)],
            s_send.at[k], s_recv.at[k], (mate, own),
        )

    def relay_copy(k):
        return copy(
            ext.at[core, 2, pl.ds(k * rows, rows)], ext.at[core, 1, pl.ds(k * rows, rows)],
            s_send.at[k], s_recv.at[k], (mate, own),
        )

    def share_copy(which, k):
        part = ext.at[core, which, pl.ds(k * rows, rows)]
        return copy(part, part, p_send.at[which - 1, k], p_recv.at[which - 1, k], (tile, other_core))

    own_copy = copy(x_ref.at[0], ext.at[core, 0], o_send, o_recv, (tile, other_core))

    for k in range(CHUNKS):
        z_copy(k).start()

        @pl.when(odd == 1)
        def _():
            first_copy(k).start()

    own_copy.start()
    ext[core, 0] = x_ref[0]

    first_row = (tile * n).astype(jnp.float32)
    row_at = lax.broadcasted_iota(jnp.int32, (8, n), 1).astype(jnp.float32)
    p = (first_row + row_at - (tiles * n - 1) / 2.0) / n
    col_at = lax.broadcasted_iota(jnp.int32, (8, blocks * n), 1).astype(jnp.float32)
    q = (col_at - (blocks * n - 1) / 2.0) / n
    for a in range(slices):
        row_cos, row_sin = cos_sin(defocus_ref[a] * (p * p))
        row_cos, row_sin = row_cos[0:1], row_sin[0:1]
        real = fr_ref[...] * row_cos - fi_ref[...] * row_sin
        imag = fr_ref[...] * row_sin + fi_ref[...] * row_cos
        left[2 * a * n : (2 * a + 1) * n, 0:n] = real.astype(jnp.bfloat16)
        left[2 * a * n : (2 * a + 1) * n, n : 2 * n] = (-imag).astype(jnp.bfloat16)
        left[(2 * a + 1) * n : (2 * a + 2) * n, 0:n] = imag.astype(jnp.bfloat16)
        left[(2 * a + 1) * n : (2 * a + 2) * n, n : 2 * n] = real.astype(jnp.bfloat16)
        c, s = cos_sin(defocus_ref[a] * (q * q))
        for j in range(pairs):
            col_cos[j, a] = c[:, j * 2 * n : (j + 1) * 2 * n]
            col_sin[j, a] = s[:, j * 2 * n : (j + 1) * 2 * n]

    def steps_of(direction, slot):
        return off_ref[direction, 0, chip * 2 + slot], off_ref[direction, 1, chip * 2 + slot]

    def taps(shape, shift, fraction, along, across):
        gap = lax.broadcasted_iota(jnp.int32, shape, along) - lax.broadcasted_iota(
            jnp.int32, shape, across
        ) - shift
        return jnp.where(gap == 0, 1.0 - fraction, jnp.where(gap == 1, fraction, 0.0)).astype(
            jnp.bfloat16
        )

    for index, direction in enumerate((other_chip, own)):
        for slot in range(2):
            row_steps, col_steps = steps_of(direction, slot)
            fy = (row_steps & (QUANT - 1)).astype(jnp.float32) * (1.0 / QUANT)
            fx = (col_steps & (QUANT - 1)).astype(jnp.float32) * (1.0 / QUANT)
            down = lax.shift_right_logical(row_steps, 2) & (n - 1)
            over = lax.shift_right_logical(col_steps, 2) & (n - 1)
            mix[index, slot] = taps((n, 2 * n), down, fy, 1, 0)
            tap = taps((3 * n, 2 * n), over, fx, 0, 1)
            for half in range(2):
                first = (slot * 2 + half) * 3 * n
                slide[index, first : first + 3 * n, :] = tap

    for k in range(CHUNKS):
        z_copy(k).wait_recv()
        share_copy(2, k).start()

        @pl.when(odd == 0)
        def _():
            relay_copy(k).start()

        first_copy(k).wait_recv()
        share_copy(1, k).start()
    own_copy.wait_recv()
    for k in range(CHUNKS):
        share_copy(2, k).wait_recv()
        share_copy(1, k).wait_recv()

    def interpolated(index, direction, store, after):
        plans = []
        for slot in range(2):
            row_steps, col_steps = steps_of(direction, slot)
            top = lax.shift_right_logical(row_steps, n.bit_length() + 1)
            plans.append((top, lax.shift_right_logical(col_steps, n.bit_length() + 1)))

        def rows_step(j, carry):
            span = pl.ds(pl.multiple_of(j * 2 * n, 2 * n), 2 * n)
            for slot in range(2):
                top = plans[slot][0]
                window = jnp.concatenate([ext[slot, top, :, span], ext[slot, top + 1, :, span]], 0)
                mixed = jnp.dot(mix[index, slot], window, preferred_element_type=jnp.float32)
                high = mixed.astype(jnp.bfloat16)
                low = (mixed - high.astype(jnp.float32)).astype(jnp.bfloat16)
                for b in range(2):
                    shifted[slot, 0, 2 * j + b] = high[:, b * n : (b + 1) * n]
                    shifted[slot, 1, 2 * j + b] = low[:, b * n : (b + 1) * n]
            return carry

        lax.fori_loop(0, pairs, rows_step, 0, unroll=4)

        def cols_step(j, carry):
            parts = []
            for slot in range(2):
                begin = plans[slot][1] + 2 * j
                for half in range(2):
                    for b in range(3):
                        parts.append(shifted[slot, half, (begin + b) & (blocks - 1)])
            total = jnp.dot(
                jnp.concatenate(parts, 1), slide[index], preferred_element_type=jnp.float32
            )
            store(j, [total[:, :n], total[:, n:]])
            after(j)
            return carry

        lax.fori_loop(0, pairs, cols_step, 0, unroll=2)

    def y_copy(j):
        return copy(send_buf.at[j], recv_buf.at[j], y_send.at[j], y_recv.at[j], (tile, other_chip))

    def store_send(j, total):
        for b in range(2):
            send_buf[j, b] = total[b].astype(jnp.bfloat16)

    def send_previous(j):
        @pl.when(j > 0)
        def _():
            y_copy(j - 1).start()

    def store_local(j, total):
        for b in range(2):
            local[j, b] = total[b]

        @pl.when(j == 0)
        def _():
            y_copy(pairs - 1).start()

    interpolated(0, other_chip, store_send, send_previous)
    interpolated(1, own, store_local, lambda j: None)

    weight_sum = weights_ref[0]
    for a in range(1, slices):
        weight_sum = weight_sum + weights_ref[a]

    def final_step(j, carry):
        y_copy(j).wait_recv()
        fields = []
        for b in range(2):
            c, s = cos_sin(local[j, b] + recv_buf[j, b].astype(jnp.float32))
            fields.append(jnp.concatenate([c, s], 0).astype(jnp.bfloat16))
        field = jnp.concatenate(fields, 1)
        sums = [jnp.zeros((n, n), jnp.float32) for _ in range(2)]
        for a in range(slices):
            focal = jnp.dot(
                left[2 * a * n : (2 * a + 2) * n, :], field, preferred_element_type=jnp.float32
            )
            real, imag = focal[:n], focal[n:]
            c, s = col_cos[j, a][0:1], col_sin[j, a][0:1]
            new_real = (real * c - imag * s).astype(jnp.bfloat16)
            new_imag = (real * s + imag * c).astype(jnp.bfloat16)
            both = jnp.concatenate(
                [
                    jnp.concatenate([new_real[:, b * n : (b + 1) * n], new_imag[:, b * n : (b + 1) * n]], 1)
                    for b in range(2)
                ],
                0,
            )
            spot = jnp.dot(both, right_ref[...], preferred_element_type=jnp.float32)
            power = spot * spot
            for b in range(2):
                piece = power[b * n : (b + 1) * n]
                sums[b] = sums[b] + weights_ref[a] * (piece[:, :n] + piece[:, n:])
        for b in range(2):
            lit = valid_ref[0, 2 * j + b].astype(jnp.float32)
            out_ref[0, 0, :, pl.ds(pl.multiple_of((2 * j + b) * n, n), n)] = (
                sums[b] / weight_sum * lit
            ).astype(jnp.bfloat16)
        return carry

    lax.fori_loop(0, pairs, final_step, 0, unroll=2)

    for k in range(CHUNKS):
        z_copy(k).wait_send()
        first_copy(k).wait_send()
        share_copy(1, k).wait_send()
        share_copy(2, k).wait_send()
    own_copy.wait_send()
    for j in range(pairs):
        y_copy(j).wait_send()


def solution(mesh):
    tiles = mesh.shape["tile"]

    def shards(layers, offsets, subap_valid, defocus, weights):
        n, cols = layers.shape[1], layers.shape[2]
        blocks = cols // n
        slices = defocus.shape[0]
        pairs = blocks // 2
        fr, fi = base_tables(n)
        right = jnp.asarray(np.block([[fr.T, fi.T], [-fi.T, fr.T]])).astype(jnp.bfloat16)
        vmem = pl.BlockSpec(memory_space=pltpu.VMEM)
        smem = pl.BlockSpec(memory_space=pltpu.SMEM)
        dma = pltpu.SemaphoreType.DMA
        return pl.pallas_call(
            functools.partial(kernel, tiles, n, blocks, slices),
            out_shape=jax.ShapeDtypeStruct((1, 1, n, cols), jnp.bfloat16),
            in_specs=[vmem, smem, smem, smem, smem, vmem, vmem, vmem],
            out_specs=vmem,
            scratch_shapes=[
                pltpu.VMEM((2, REACH + 1, n, cols), jnp.bfloat16),
                pltpu.VMEM((2, 2, blocks, n, n), jnp.bfloat16),
                pltpu.VMEM((2, 2, n, 2 * n), jnp.bfloat16),
                pltpu.VMEM((2, 12 * n, 2 * n), jnp.bfloat16),
                pltpu.VMEM((pairs, 2, n, n), jnp.bfloat16),
                pltpu.VMEM((pairs, 2, n, n), jnp.bfloat16),
                pltpu.VMEM((pairs, 2, n, n), jnp.float32),
                pltpu.VMEM((2 * slices * n, 2 * n), jnp.bfloat16),
                pltpu.VMEM((pairs, slices, 8, 2 * n), jnp.float32),
                pltpu.VMEM((pairs, slices, 8, 2 * n), jnp.float32),
                dma((CHUNKS,)), dma((CHUNKS,)),
                dma((CHUNKS,)), dma((CHUNKS,)),
                dma, dma,
                dma((REACH, CHUNKS)), dma((REACH, CHUNKS)),
                dma((pairs,)), dma((pairs,)),
            ],
            compiler_params=pltpu.CompilerParams(collective_id=0, has_side_effects=True),
        )(layers, jnp.transpose(offsets, (0, 2, 1)), subap_valid, defocus, weights, jnp.asarray(fr), jnp.asarray(fi), right)

    placed = (P("dir", "tile", None), P(), P("tile", None), P(), P())
    return jax.shard_map(
        shards, mesh=mesh, in_specs=placed, out_specs=P("dir", "tile", None, None), check_vma=False
    )
```

profile of v0, /device:TPU:2, one launch (start us, length us, event | category | flops | bytes accessed | tf_op | source)
XLA Modules:
  0.0 39.3 jit_solution(17651969129899497013)
XLA Ops:
  0.0 37.4 %shard_map.82 = bf16[1,1,128,2048]{3,2,1,0:T(8,128)(2,1)} custom-call(bf16[1,128,2048]{2,1,0:T(8,128)(2,1)} %x_ref.1, s32[4,2,4]{2,1,0:T(2,128)} %bitcast.1, s32[1,16]{1,0:T(1,128)} %valid_ref.1, f32[3]{0:T(128)} %defocus_ref.1, f32[3]{0:T(128)} %weights_ref.1, f32[128,128]{1,0:T(8,128)} %constant.7.clone.fr_ref, f32[128,128]{1,0:T(8,128)} %constant.8.clone.fi_ref, ...), custom_call_target="tpu_custom_call" | custom-call | tf_op jit(solution)/shard_map/pallas_call | solution.py:294
  37.4 1.9 %copy.10 = bf16[1,1,128,2048]{3,2,1,0:T(8,128)(2,1)} copy(bf16[1,1,128,2048]{3,2,1,0:T(8,128)(2,1)} %shard_map.82) | data formatting | bytes 1048576
where the time goes:
time: 40.1 us; the launch traced here: 39.3 us
  Pallas kernels  37.4 us (93%)
  local copies, waits for them, and re-layouts  1.88 us (5%)
    pallas_call x1, Pallas kernels, shards(): pl.pallas_call(functools.partial(kernel, tiles, n, blocks, slices), out_s...  37.4 us
    unnamed x1, local copies, waits for them, and re-layouts  1.88 us

commit v1 on v0

--- a/solution.py
+++ b/solution.py
@@ -293,7 +293,7 @@
         dma = pltpu.SemaphoreType.DMA
         return pl.pallas_call(
             functools.partial(kernel, tiles, n, blocks, slices),
-            out_shape=jax.ShapeDtypeStruct((1, 1, n, cols), jnp.bfloat16),
+            out_shape=pltpu.VMEM((1, 1, n, cols), jnp.bfloat16),
             in_specs=[vmem, smem, smem, smem, smem, vmem, vmem, vmem],
             out_specs=vmem,
             scratch_shapes=[

time: 40.1 us -> 38.2 us (0.953)
  local copies, waits for them, and re-layouts: 1.88 us -> 0.8 us
  Pallas kernels: 37.4 us -> 36.6 us
    unnamed x1, local copies, waits for them, and re-layouts: 1.88 us -> 0.8 us
    pallas_call x1, Pallas kernels: 37.4 us -> 36.6 us  [shards(): pl.pallas_call(functools.partial(kernel, tiles, n, blocks, slices), out_s...]
where the time goes in v1:
time: 38.2 us; the launch traced here: 37.4 us
  Pallas kernels  36.6 us (96%)
  local copies, waits for them, and re-layouts  0.8 us (2%)
    pallas_call x1, Pallas kernels, shards(): pl.pallas_call(functools.partial(kernel, tiles, n, blocks, slices), out_s...  36.6 us
    unnamed x1, local copies, waits for them, and re-layouts  0.8 us

profile of v1, /device:TPU:2, one launch (start us, length us, event | category | flops | bytes accessed | tf_op | source)
XLA Modules:
  0.0 37.4 jit_solution(10191823004506237951)
XLA Ops:
  0.0 36.6 %shard_map.82 = bf16[1,1,128,2048]{3,2,1,0:T(8,128)(2,1)S(1)} custom-call(bf16[1,128,2048]{2,1,0:T(8,128)(2,1)} %x_ref.1, s32[4,2,4]{2,1,0:T(2,128)} %bitcast.1, s32[1,16]{1,0:T(1,128)} %valid_ref.1, f32[3]{0:T(128)} %defocus_ref.1, f32[3]{0:T(128)} %weights_ref.1, f32[128,128]{1,0:T(8,128)} %constant.7.clone.fr_ref, f32[128,128]{1,0:T(8,128)} %constant.8.clone.fi_ref, ...), custom_call_target="tpu_custom_call" | custom-call | tf_op jit(solution)/shard_map/pallas_call | solution.py:294
  36.6 0.8 %copy.10 = bf16[1,1,128,2048]{3,2,1,0:T(8,128)(2,1)} copy(bf16[1,1,128,2048]{3,2,1,0:T(8,128)(2,1)S(1)} %shard_map.82) | data formatting | bytes 1048576

commit v2 on v1

v2 whole, which is shorter than its diff:
```python
import functools
import math

import jax
import jax.numpy as jnp
import numpy as np
from jax import lax
from jax.experimental import pallas as pl
from jax.experimental.pallas import tpu as pltpu
from jax.sharding import PartitionSpec as P

OVER = 2
QUANT = 4
REACH = 2
GROUP = 4
MESH = pl.DeviceIdType.MESH
HALF_PI_HI = 1.5703125
HALF_PI_LO = math.pi / 2 - 1.5703125


def base_tables(n):
    frequency = np.arange(n, dtype=np.float64) - n // 2
    position = np.arange(n, dtype=np.float64) - (n - 1) / 2.0
    angle = -2.0 * math.pi / (OVER * n) * frequency[:, None] * position[None, :]
    factor = 1.0 / math.sqrt(n)
    return (np.cos(angle) * factor).astype(np.float32), (np.sin(angle) * factor).astype(np.float32)


def cos_sin(angle):
    turns = jnp.round(angle * (2.0 / math.pi))
    rest = (angle - turns * HALF_PI_HI) - turns * HALF_PI_LO
    quadrant = turns.astype(jnp.int32)
    square = rest * rest
    sin = rest + rest * square * (-1.0 / 6 + square * (1.0 / 120 - square * (1.0 / 5040)))
    cos = 1.0 + square * (-0.5 + square * (1.0 / 24 - square * (1.0 / 720 - square * (1.0 / 40320))))
    swap = (quadrant & 1) == 1
    cos_value = jnp.where(swap, sin, cos)
    sin_value = jnp.where(swap, cos, sin)
    cos_value = jnp.where(((quadrant + 1) & 2) == 2, -cos_value, cos_value)
    sin_value = jnp.where((quadrant & 2) == 2, -sin_value, sin_value)
    return cos_value, sin_value


def taps(shape, shift, fraction, along, across):
    gap = lax.broadcasted_iota(jnp.int32, shape, along) - lax.broadcasted_iota(
        jnp.int32, shape, across
    ) - shift
    return jnp.where(gap == 0, 1.0 - fraction, jnp.where(gap == 1, fraction, 0.0)).astype(
        jnp.bfloat16
    )


def kernel(
    tiles, n, blocks, slices,
    x_ref, off_ref, valid_ref, defocus_ref, weights_ref, fr_ref, fi_ref, right_ref,
    out_ref,
    own, twin, far, halo, mixed, moved, front_mix, front_slide, back_mix, back_slide,
    x_buf, x_in, tail, out_buf, in_buf, local, left, col_cos, col_sin, fr_tab, fi_tab, right_tab,
    load_sem, table_sem, z_send, z_recv, f_send, r_send, h_recv, y_send, y_recv, t_send, t_recv,
    x_send, x_recv, o_send, o_recv, ready,
):
    tile = lax.axis_index("tile")
    place = lax.axis_index("dir")
    core = lax.rem(place, 2)
    chip = lax.div(place, 2)
    partner = chip * 2 + (1 - core)
    front, back = chip * 2, chip * 2 + 1
    far_front, far_back = (1 - chip) * 2, (1 - chip) * 2 + 1
    odd = lax.rem(tile, 2)
    mate = tile + 1 - 2 * odd
    below = lax.rem(tile + tiles - 2, tiles)
    above = lax.rem(tile + 2, tiles)
    pairs = blocks // 2
    is_front, is_back = core == 0, core == 1

    barrier = pltpu.get_barrier_semaphore()

    def greet(device):
        pl.semaphore_signal(barrier, inc=1, device_id=device, device_id_type=MESH)

    first, last = tile < 2, tile >= tiles - 2

    @pl.when(jnp.logical_not(last))
    def _():
        greet((above, front + core))

        @pl.when(is_back)
        def _():
            greet((above, front))

    @pl.when(first)
    def _():
        greet((below, back))

        @pl.when(is_front)
        def _():
            greet((below, front))

    @pl.when(is_front)
    def _():
        greet((tile, far_back))

    @pl.when(is_back)
    def _():
        @pl.when(odd == 0)
        def _():
            greet((mate, front))

    greet((mate, front + core))
    greet((tile, far_front + core))
    greet((tile, partner))

    def load(k):
        return pltpu.make_async_copy(
            x_ref.at[0, :, pl.ds(k * n, n)], own.at[k], load_sem.at[k]
        )

    tables = [
        pltpu.make_async_copy(source, target, table_sem.at[i])
        for i, (source, target) in enumerate(
            ((fr_ref, fr_tab), (fi_ref, fi_tab), (right_ref, right_tab))
        )
    ]
    for k in range(blocks):
        load(k).start()
    for table in tables:
        table.start()

    def copy(source, target, send, recv, device):
        return pltpu.make_async_remote_copy(
            src_ref=source, dst_ref=target, send_sem=send, recv_sem=recv,
            device_id=device, device_id_type=MESH,
        )

    def z_copy(k, layer=core):
        return copy(own.at[k], halo.at[layer, 1, k], z_send.at[k], z_recv.at[layer, k], (below, back))

    def f_copy(k, layer=core):
        return copy(own.at[k], halo.at[layer, 0, k], f_send.at[k], h_recv.at[layer, k], (mate, back))

    def relay(k, layer):
        return copy(
            halo.at[layer, 1, k], halo.at[layer, 0, k], r_send.at[layer, k], h_recv.at[layer, k],
            (mate, back),
        )

    def far_copy(layer=core):
        return copy(own, far.at[layer], y_send, y_recv.at[layer], (tile, far_front))

    twin_copy = copy(own, twin, t_send, t_recv, (tile, partner))

    def x_copy(j):
        return copy(x_buf.at[j], x_in.at[j], x_send.at[j], x_recv.at[j], (mate, front))

    def down_copy(j):
        return copy(out_buf.at[j], in_buf.at[j], o_send.at[j], o_recv.at[j], (below, front))

    def across_copy(j):
        return copy(out_buf.at[j], in_buf.at[j], o_send.at[j], o_recv.at[j], (tile, far_back))

    downward = jnp.where(is_front, 2, 1)
    upward = jnp.where(is_front, 1, 2)
    pl.semaphore_wait(
        barrier,
        5 + jnp.where(is_front, odd, 0) - jnp.where(first, downward, 0) + jnp.where(last, upward, 0),
    )

    @pl.when(last)
    def _():
        def answer(device):
            pl.semaphore_signal(ready, inc=1, device_id=device, device_id_type=MESH)

        answer((above, front))

        @pl.when(is_back)
        def _():
            answer((above, back))

    for k in range(blocks):
        load(k).wait()

        @pl.when(jnp.logical_not(first))
        def _():
            z_copy(k).start()

        @pl.when(odd == 1)
        def _():
            f_copy(k).start()

    far_copy().start()
    twin_copy.start()
    for table in tables:
        table.wait()

    first_row = (tile * n).astype(jnp.float32)
    row_at = lax.broadcasted_iota(jnp.int32, (8, n), 1).astype(jnp.float32)
    p = (first_row + row_at - (tiles * n - 1) / 2.0) / n
    col_at = lax.broadcasted_iota(jnp.int32, (8, blocks * n), 1).astype(jnp.float32)
    q = (col_at - (blocks * n - 1) / 2.0) / n
    for a in range(slices):
        row_cos, row_sin = cos_sin(defocus_ref[a] * (p * p))
        row_cos, row_sin = row_cos[0:1], row_sin[0:1]
        real = fr_tab[...] * row_cos - fi_tab[...] * row_sin
        imag = fr_tab[...] * row_sin + fi_tab[...] * row_cos
        left[2 * a * n : (2 * a + 1) * n, 0:n] = real.astype(jnp.bfloat16)
        left[2 * a * n : (2 * a + 1) * n, n : 2 * n] = (-imag).astype(jnp.bfloat16)
        left[(2 * a + 1) * n : (2 * a + 2) * n, 0:n] = imag.astype(jnp.bfloat16)
        left[(2 * a + 1) * n : (2 * a + 2) * n, n : 2 * n] = real.astype(jnp.bfloat16)
        c, s = cos_sin(defocus_ref[a] * (q * q))
        for j in range(pairs):
            col_cos[j, a] = c[:, j * 2 * n : (j + 1) * 2 * n]
            col_sin[j, a] = s[:, j * 2 * n : (j + 1) * 2 * n]

    @pl.when(first)
    def _():
        pl.semaphore_wait(ready, downward)
        for k in range(blocks):
            z_copy(k).start()

    def plan_of(direction, layer):
        row_steps, col_steps = off_ref[direction, 0, layer], off_ref[direction, 1, layer]
        fy = (row_steps & (QUANT - 1)).astype(jnp.float32) * (1.0 / QUANT)
        fx = (col_steps & (QUANT - 1)).astype(jnp.float32) * (1.0 / QUANT)
        down = lax.shift_right_logical(row_steps, 2)
        over = lax.shift_right_logical(col_steps, 2) & (n - 1)
        begin = lax.shift_right_logical(col_steps, n.bit_length() + 1)
        return down, fy, over, fx, begin

    @pl.when(is_front)
    def _():
        plans = [
            plan_of(place, layer)
            for layer in (front, back, far_front, far_back)
        ]
        for slot, (down, fy, over, fx, _) in enumerate(plans):
            front_slide[slot] = taps((3 * n, 2 * n), over, fx, 0, 1)
            for reach in range(REACH + 1):
                front_mix[reach * n : (reach + 1) * n, slot * n : (slot + 1) * n] = taps(
                    (n, n), down - reach * n, fy, 1, 0
                )

        def shift(slot, block_of):
            begin = plans[slot][4]

            def step(g, carry):
                rows = []
                for j in range(GROUP):
                    at = begin + 2 * (g * GROUP + j)
                    rows.append(
                        jnp.concatenate([block_of((at + b) & (blocks - 1)) for b in range(3)], 1)
                    )
                total = jnp.dot(
                    jnp.concatenate(rows, 0), front_slide[slot], preferred_element_type=jnp.float32
                ).astype(jnp.bfloat16)
                for j in range(GROUP):
                    mixed[g * GROUP + j, slot * n : (slot + 1) * n, :] = total[j * n : (j + 1) * n]
                return carry

            lax.fori_loop(0, pairs // GROUP, step, 0)

        shift(0, lambda b: own[b])
        twin_copy.wait_recv()
        shift(1, lambda b: twin[b])
        for layer in range(2):
            far_copy(layer).wait_recv()
        for layer in range(2):
            shift(2 + layer, lambda b: far[layer, b])

        def give_step(j, carry):
            total = jnp.dot(front_mix[...], mixed[j], preferred_element_type=jnp.float32)
            local[j] = total[:n]
            x_buf[j] = total[n : 2 * n].astype(jnp.bfloat16)
            tail[j] = total[2 * n :]
            out_buf[j] = total[2 * n :].astype(jnp.bfloat16)

            @pl.when(j > 0)
            def _():
                x_copy(j - 1).start()

            @pl.when((j > 0) & (odd == 0))
            def _():
                down_copy(j - 1).start()

            return carry

        lax.fori_loop(0, pairs, give_step, 0, unroll=2)
        x_copy(pairs - 1).start()

        @pl.when(odd == 0)
        def _():
            down_copy(pairs - 1).start()

        @pl.when(odd == 1)
        def _():
            def pass_step(j, carry):
                x_copy(j).wait_recv()
                out_buf[j] = (tail[j] + x_in[j].astype(jnp.float32)).astype(jnp.bfloat16)

                @pl.when(j > 0)
                def _():
                    down_copy(j - 1).start()

                return carry

            lax.fori_loop(0, pairs, pass_step, 0)
            down_copy(pairs - 1).start()

    @pl.when(is_back)
    def _():
        plans = [
            [plan_of(direction, layer) for layer in (front, back)]
            for direction in (far_back, place)
        ]
        for index in range(2):
            for slot in range(2):
                down, fy, over, fx, _ = plans[index][slot]
                back_mix[slot, index * n : (index + 1) * n, :] = taps((n, 3 * n), down, fy, 1, 0)
                back_slide[index, slot * 3 * n : (slot + 1) * 3 * n, :] = taps(
                    (3 * n, 2 * n), over, fx, 0, 1
                )
        twin_copy.wait_recv()

        def rows_step(j, carry):
            for b in range(2):
                for layer in range(2):
                    z_copy(2 * j + b, layer).wait_recv()

                    @pl.when(odd == 0)
                    def _():
                        relay(2 * j + b, layer).start()

            for layer in range(2):
                nearest = twin if layer == 0 else own
                for b in range(2):
                    relay(2 * j + b, layer).wait_recv()
                window = jnp.concatenate(
                    [
                        jnp.concatenate(
                            [nearest[2 * j + b], halo[layer, 0, 2 * j + b], halo[layer, 1, 2 * j + b]], 0
                        )
                        for b in range(2)
                    ],
                    1,
                )
                total = jnp.dot(
                    back_mix[layer], window, preferred_element_type=jnp.float32
                ).astype(jnp.bfloat16)
                for index in range(2):
                    for b in range(2):
                        moved[layer, index, 2 * j + b] = total[
                            index * n : (index + 1) * n, b * n : (b + 1) * n
                        ]
            return carry

        lax.fori_loop(0, pairs, rows_step, 0)

        def cols(index, j):
            parts = []
            for layer in range(2):
                begin = plans[index][layer][4] + 2 * j
                for b in range(3):
                    parts.append(moved[layer, index, (begin + b) & (blocks - 1)])
            return jnp.dot(
                jnp.concatenate(parts, 1), back_slide[index], preferred_element_type=jnp.float32
            )

        def give_step(j, carry):
            out_buf[j] = cols(0, j).astype(jnp.bfloat16)

            @pl.when(j > 0)
            def _():
                across_copy(j - 1).start()

            return carry

        lax.fori_loop(0, pairs, give_step, 0, unroll=2)

        def keep_step(j, carry):
            local[j] = cols(1, j)

            @pl.when(j == 0)
            def _():
                across_copy(pairs - 1).start()

            return carry

        lax.fori_loop(0, pairs, keep_step, 0, unroll=2)

    weight_sum = weights_ref[0]
    for a in range(1, slices):
        weight_sum = weight_sum + weights_ref[a]

    def final_step(j, carry):
        across_copy(j).wait_recv()

        @pl.when(is_front & (odd == 0))
        def _():
            x_copy(j).wait_recv()
            local[j] = local[j] + x_in[j].astype(jnp.float32)

        c, s = cos_sin(local[j] + in_buf[j].astype(jnp.float32))
        field = jnp.concatenate([c, s], 0).astype(jnp.bfloat16)
        sums = [jnp.zeros((n, n), jnp.float32) for _ in range(2)]
        for a in range(slices):
            focal = jnp.dot(
                left[2 * a * n : (2 * a + 2) * n, :], field, preferred_element_type=jnp.float32
            )
            real, imag = focal[:n], focal[n:]
            c, s = col_cos[j, a][0:1], col_sin[j, a][0:1]
            new_real = (real * c - imag * s).astype(jnp.bfloat16)
            new_imag = (real * s + imag * c).astype(jnp.bfloat16)
            both = jnp.concatenate(
                [
                    jnp.concatenate([new_real[:, b * n : (b + 1) * n], new_imag[:, b * n : (b + 1) * n]], 1)
                    for b in range(2)
                ],
                0,
            )
            spot = jnp.dot(both, right_tab[...], preferred_element_type=jnp.float32)
            power = spot * spot
            for b in range(2):
                piece = power[b * n : (b + 1) * n]
                sums[b] = sums[b] + weights_ref[a] * (piece[:, :n] + piece[:, n:])
        for b in range(2):
            lit = valid_ref[0, 2 * j + b].astype(jnp.float32)
            out_ref[0, 0, :, pl.ds(pl.multiple_of((2 * j + b) * n, n), n)] = (
                sums[b] / weight_sum * lit
            ).astype(jnp.bfloat16)
        return carry

    lax.fori_loop(0, pairs, final_step, 0, unroll=2)

    for k in range(blocks):
        z_copy(k).wait_send()

    @pl.when(odd == 1)
    def _():
        for k in range(blocks):
            f_copy(k).wait_send()

    far_copy().wait_send()
    twin_copy.wait_send()
    for j in range(pairs):
        across_copy(j).wait_send()

    @pl.when(is_front)
    def _():
        for j in range(pairs):
            x_copy(j).wait_send()

    @pl.when(is_back & (odd == 0))
    def _():
        for k in range(blocks):
            for layer in range(2):
                relay(k, layer).wait_send()


def solution(mesh):
    tiles = mesh.shape["tile"]

    def shards(layers, offsets, subap_valid, defocus, weights):
        n, cols = layers.shape[1], layers.shape[2]
        blocks = cols // n
        slices = defocus.shape[0]
        pairs = blocks // 2
        fr, fi = base_tables(n)
        right = jnp.asarray(np.block([[fr.T, fi.T], [-fi.T, fr.T]])).astype(jnp.bfloat16)
        vmem = pl.BlockSpec(memory_space=pltpu.VMEM)
        smem = pl.BlockSpec(memory_space=pltpu.SMEM)
        hbm = pl.BlockSpec(memory_space=pl.ANY)
        dma = pltpu.SemaphoreType.DMA
        half, full = jnp.bfloat16, jnp.float32
        return pl.pallas_call(
            functools.partial(kernel, tiles, n, blocks, slices),
            out_shape=pltpu.VMEM((1, 1, n, cols), half),
            in_specs=[hbm, smem, smem, smem, smem, hbm, hbm, hbm],
            out_specs=vmem,
            scratch_shapes=[
                pltpu.VMEM((blocks, n, n), half),
                pltpu.VMEM((blocks, n, n), half),
                pltpu.VMEM((2, blocks, n, n), half),
                pltpu.VMEM((2, REACH, blocks, n, n), half),
                pltpu.VMEM((pairs, 4 * n, 2 * n), half),
                pltpu.VMEM((2, 2, blocks, n, n), half),
                pltpu.VMEM(((REACH + 1) * n, 4 * n), half),
                pltpu.VMEM((4, 3 * n, 2 * n), half),
                pltpu.VMEM((2, 2 * n, (REACH + 1) * n), half),
                pltpu.VMEM((2, 6 * n, 2 * n), half),
                pltpu.VMEM((pairs, n, 2 * n), half),
                pltpu.VMEM((pairs, n, 2 * n), half),
                pltpu.VMEM((pairs, n, 2 * n), full),
                pltpu.VMEM((pairs, n, 2 * n), half),
                pltpu.VMEM((pairs, n, 2 * n), half),
                pltpu.VMEM((pairs, n, 2 * n), full),
                pltpu.VMEM((2 * slices * n, 2 * n), half),
                pltpu.VMEM((pairs, slices, 8, 2 * n), full),
                pltpu.VMEM((pairs, slices, 8, 2 * n), full),
                pltpu.VMEM((n, n), full),
                pltpu.VMEM((n, n), full),
                pltpu.VMEM((2 * n, 2 * n), half),
                dma((blocks,)), dma((3,)),
                dma((blocks,)), dma((2, blocks)),
                dma((blocks,)), dma((2, blocks)), dma((2, blocks)),
                dma, dma((2,)),
                dma, dma,
                dma((pairs,)), dma((pairs,)),
                dma((pairs,)), dma((pairs,)),
                pltpu.SemaphoreType.REGULAR,
            ],
            compiler_params=pltpu.CompilerParams(collective_id=0, has_side_effects=True),
        )(layers, jnp.transpose(offsets, (0, 2, 1)), subap_valid, defocus, weights, jnp.asarray(fr), jnp.asarray(fi), right)

    placed = (P("dir", "tile", None), P(), P("tile", None), P(), P())
    return jax.shard_map(
        shards, mesh=mesh, in_specs=placed, out_specs=P("dir", "tile", None, None), check_vma=False
    )
```

time: 38.2 us -> 35.1 us (0.919)
  the two profiles are of different devices: /device:TPU:2 before, /device:TPU:31 now
where the time goes in v2:
time: 35.1 us; the launch traced here: 34.9 us
  Pallas kernels  34.1 us (97%)
  local copies, waits for them, and re-layouts  0.8 us (2%)
    pallas_call x1, Pallas kernels, shards(): pl.pallas_call(functools.partial(kernel, tiles, n, blocks, slices), out_s...  34.1 us
    unnamed x1, local copies, waits for them, and re-layouts  0.8 us

profile of v2, /device:TPU:31, one launch (start us, length us, event | category | flops | bytes accessed | tf_op | source)
XLA Modules:
  0.0 34.9 jit_solution(7488797125453250523)
XLA Ops:
  0.0 34.1 %shard_map.82 = bf16[1,1,128,2048]{3,2,1,0:T(8,128)(2,1)S(1)} custom-call(bf16[1,128,2048]{2,1,0:T(8,128)(2,1)} %x_ref.1, s32[4,2,4]{2,1,0:T(2,128)} %bitcast.1, s32[1,16]{1,0:T(1,128)} %valid_ref.1, f32[3]{0:T(128)} %defocus_ref.1, f32[3]{0:T(128)} %weights_ref.1, f32[128,128]{1,0:T(8,128)} %constant.7.clone.fr_ref, f32[128,128]{1,0:T(8,128)} %constant.8.clone.fi_ref, ...), custom_call_target="tpu_custom_call" | custom-call | tf_op jit(solution)/shard_map/pallas_call | solution.py:473
  34.1 0.8 %copy.10 = bf16[1,1,128,2048]{3,2,1,0:T(8,128)(2,1)} copy(bf16[1,1,128,2048]{3,2,1,0:T(8,128)(2,1)S(1)} %shard_map.82) | data formatting | bytes 1048576

commit v3 on v2

--- a/solution.py
+++ b/solution.py
@@ -13,9 +13,10 @@
 QUANT = 4
 REACH = 2
 GROUP = 4
+AHEAD = 8
 MESH = pl.DeviceIdType.MESH
-HALF_PI_HI = 1.5703125
-HALF_PI_LO = math.pi / 2 - 1.5703125
+SIN = (3.141582022082025, -5.167142794167084, 2.541899009948703, -0.5546361567315732)
+COS = (0.999999953466345, -4.934792858633932, 4.058411913339297, -1.3318801559459539, 0.21969678799073292)
 
 
 def base_tables(n):
@@ -27,18 +28,17 @@
 
 
 def cos_sin(angle):
-    turns = jnp.round(angle * (2.0 / math.pi))
-    rest = (angle - turns * HALF_PI_HI) - turns * HALF_PI_LO
-    quadrant = turns.astype(jnp.int32)
+    turns = angle * (1.0 / math.pi)
+    whole = jnp.round(turns)
+    rest = turns - whole
+    sign = jnp.where((whole.astype(jnp.int32) & 1) == 0, 1.0, -1.0)
     square = rest * rest
-    sin = rest + rest * square * (-1.0 / 6 + square * (1.0 / 120 - square * (1.0 / 5040)))
-    cos = 1.0 + square * (-0.5 + square * (1.0 / 24 - square * (1.0 / 720 - square * (1.0 / 40320))))
-    swap = (quadrant & 1) == 1
-    cos_value = jnp.where(swap, sin, cos)
-    sin_value = jnp.where(swap, cos, sin)
-    cos_value = jnp.where(((quadrant + 1) & 2) == 2, -cos_value, cos_value)
-    sin_value = jnp.where((quadrant & 2) == 2, -sin_value, sin_value)
-    return cos_value, sin_value
+    sin, cos = SIN[-1], COS[-1]
+    for factor in SIN[-2::-1]:
+        sin = factor + square * sin
+    for factor in COS[-2::-1]:
+        cos = factor + square * cos
+    return cos * sign, sin * (rest * sign)
 
 
 def taps(shape, shift, fraction, along, across):
@@ -52,10 +52,10 @@
 
 def kernel(
     tiles, n, blocks, slices,
-    x_ref, off_ref, valid_ref, defocus_ref, weights_ref, fr_ref, fi_ref, right_ref,
+    x_ref, off_hbm, valid_hbm, defocus_hbm, weights_hbm, base_ref, right_ref,
     out_ref,
-    own, twin, far, halo, mixed, moved, front_mix, front_slide, back_mix, back_slide,
-    x_buf, x_in, tail, out_buf, in_buf, local, left, col_cos, col_sin, fr_tab, fi_tab, right_tab,
+    off_ref, valid_ref, defocus_ref, weights_ref, own, twin, far, halo, mixed, moved, front_mix, front_slide, back_mix, back_slide,
+    x_buf, x_in, tail, out_buf, in_buf, local, left, col_cos, col_sin, base_tab, right_tab,
     load_sem, table_sem, z_send, z_recv, f_send, r_send, h_recv, y_send, y_recv, t_send, t_recv,
     x_send, x_recv, o_send, o_recv, ready,
 ):
@@ -110,19 +110,17 @@
     greet((tile, far_front + core))
     greet((tile, partner))
 
-    def load(k):
-        return pltpu.make_async_copy(
-            x_ref.at[0, :, pl.ds(k * n, n)], own.at[k], load_sem.at[k]
-        )
-
+    for k in range(blocks):
+        pltpu.make_async_copy(x_ref.at[0, :, pl.ds(k * n, n)], own.at[k], load_sem).start()
     tables = [
         pltpu.make_async_copy(source, target, table_sem.at[i])
         for i, (source, target) in enumerate(
-            ((fr_ref, fr_tab), (fi_ref, fi_tab), (right_ref, right_tab))
+            (
+                (defocus_hbm, defocus_ref), (off_hbm, off_ref), (weights_hbm, weights_ref),
+                (valid_hbm, valid_ref), (base_ref, base_tab), (right_ref, right_tab),
+            )
         )
     ]
-    for k in range(blocks):
-        load(k).start()
     for table in tables:
         table.start()
 
@@ -132,31 +130,59 @@
             device_id=device, device_id_type=MESH,
         )
 
-    def z_copy(k, layer=core):
-        return copy(own.at[k], halo.at[layer, 1, k], z_send.at[k], z_recv.at[layer, k], (below, back))
-
-    def f_copy(k, layer=core):
-        return copy(own.at[k], halo.at[layer, 0, k], f_send.at[k], h_recv.at[layer, k], (mate, back))
-
-    def relay(k, layer):
+    def pair_of(k):
+        return pl.ds(2 * k, 2)
+
+    def z_copy(k):
         return copy(
-            halo.at[layer, 1, k], halo.at[layer, 0, k], r_send.at[layer, k], h_recv.at[layer, k],
-            (mate, back),
+            own.at[pair_of(k)], halo.at[core, 1, pair_of(k)], z_send, z_recv.at[k], (below, back)
         )
 
-    def far_copy(layer=core):
-        return copy(own, far.at[layer], y_send, y_recv.at[layer], (tile, far_front))
+    def f_copy(k):
+        return copy(
+            own.at[pair_of(k)], halo.at[core, 0, pair_of(k)], f_send, h_recv.at[k], (mate, back)
+        )
+
+    def relay(k):
+        return copy(
+            halo.at[:, 1, pair_of(k)], halo.at[:, 0, pair_of(k)], r_send, h_recv.at[k], (mate, back)
+        )
+
+    def z_both(k):
+        part = halo.at[:, 1, pair_of(k)]
+        return copy(part, part, r_send, z_recv.at[k], (mate, back))
+
+    z_all = copy(own, halo.at[core, 1], z_send, z_recv.at[0], (below, back))
+    f_all = copy(own, halo.at[core, 0], f_send, h_recv.at[0], (mate, back))
+    r_all = copy(halo.at[:, 1], halo.at[:, 0], r_send, h_recv.at[0], (mate, back))
+    far_copy = copy(own, far.at[core], y_send, y_recv, (tile, far_front))
+    far_both = copy(far, far, y_send, y_recv, (tile, far_front))
 
     twin_copy = copy(own, twin, t_send, t_recv, (tile, partner))
 
     def x_copy(j):
-        return copy(x_buf.at[j], x_in.at[j], x_send.at[j], x_recv.at[j], (mate, front))
+        return copy(x_buf.at[j], x_in.at[j], x_send, x_recv.at[j], (mate, front))
 
     def down_copy(j):
-        return copy(out_buf.at[j], in_buf.at[j], o_send.at[j], o_recv.at[j], (below, front))
+        return copy(out_buf.at[j], in_buf.at[j], o_send, o_recv.at[j], (below, front))
+
+    def pass_on(j):
+        for b in range(2):
+            k = 2 * j + b
+            x_copy(k).wait_recv()
+            out_buf[k] = (
+                tail[j, :, b * n : (b + 1) * n] + x_in[k].astype(jnp.float32)
+            ).astype(jnp.bfloat16)
+
+            @pl.when(k > 0)
+            def _():
+                down_copy(k - 1).start()
 
     def across_copy(j):
-        return copy(out_buf.at[j], in_buf.at[j], o_send.at[j], o_recv.at[j], (tile, far_back))
+        return copy(out_buf.at[j], in_buf.at[j], o_send, o_recv.at[j], (tile, far_back))
+
+    x_all = copy(x_buf, x_in, x_send, x_recv.at[0], (mate, front))
+    out_all = copy(out_buf, in_buf, o_send, o_recv.at[0], (tile, far_back))
 
     downward = jnp.where(is_front, 2, 1)
     upward = jnp.where(is_front, 1, 2)
@@ -176,8 +202,8 @@
         def _():
             answer((above, back))
 
-    for k in range(blocks):
-        load(k).wait()
+    pltpu.make_async_copy(twin, own, load_sem).wait()
+    for k in range(pairs):
 
         @pl.when(jnp.logical_not(first))
         def _():
@@ -187,7 +213,7 @@
         def _():
             f_copy(k).start()
 
-    far_copy().start()
+    far_copy.start()
     twin_copy.start()
     for table in tables:
         table.wait()
@@ -200,8 +226,8 @@
     for a in range(slices):
         row_cos, row_sin = cos_sin(defocus_ref[a] * (p * p))
         row_cos, row_sin = row_cos[0:1], row_sin[0:1]
-        real = fr_tab[...] * row_cos - fi_tab[...] * row_sin
-        imag = fr_tab[...] * row_sin + fi_tab[...] * row_cos
+        real = base_tab[0] * row_cos - base_tab[1] * row_sin
+        imag = base_tab[0] * row_sin + base_tab[1] * row_cos
         left[2 * a * n : (2 * a + 1) * n, 0:n] = real.astype(jnp.bfloat16)
         left[2 * a * n : (2 * a + 1) * n, n : 2 * n] = (-imag).astype(jnp.bfloat16)
         left[(2 * a + 1) * n : (2 * a + 2) * n, 0:n] = imag.astype(jnp.bfloat16)
@@ -214,7 +240,7 @@
     @pl.when(first)
     def _():
         pl.semaphore_wait(ready, downward)
-        for k in range(blocks):
+        for k in range(pairs):
             z_copy(k).start()
 
     def plan_of(direction, layer):
@@ -261,49 +287,50 @@
         shift(0, lambda b: own[b])
         twin_copy.wait_recv()
         shift(1, lambda b: twin[b])
-        for layer in range(2):
-            far_copy(layer).wait_recv()
+        far_both.wait_recv()
         for layer in range(2):
             shift(2 + layer, lambda b: far[layer, b])
 
         def give_step(j, carry):
             total = jnp.dot(front_mix[...], mixed[j], preferred_element_type=jnp.float32)
             local[j] = total[:n]
-            x_buf[j] = total[n : 2 * n].astype(jnp.bfloat16)
             tail[j] = total[2 * n :]
-            out_buf[j] = total[2 * n :].astype(jnp.bfloat16)
-
-            @pl.when(j > 0)
-            def _():
-                x_copy(j - 1).start()
+            for b in range(2):
+                part = slice(b * n, (b + 1) * n)
+                x_buf[2 * j + b] = total[n : 2 * n, part].astype(jnp.bfloat16)
+                out_buf[2 * j + b] = total[2 * n :, part].astype(jnp.bfloat16)
 
             @pl.when((j > 0) & (odd == 0))
             def _():
-                down_copy(j - 1).start()
+                for b in range(2):
+                    down_copy(2 * j - 2 + b).start()
+
+            @pl.when((j > 0) & (odd == 1))
+            def _():
+                for b in range(2):
+                    x_copy(2 * j - 2 + b).start()
 
             return carry
 
         lax.fori_loop(0, pairs, give_step, 0, unroll=2)
-        x_copy(pairs - 1).start()
 
         @pl.when(odd == 0)
         def _():
-            down_copy(pairs - 1).start()
+            for b in range(2):
+                down_copy(blocks - 2 + b).start()
+            for k in range(blocks):
+                x_copy(k).start()
 
         @pl.when(odd == 1)
         def _():
-            def pass_step(j, carry):
-                x_copy(j).wait_recv()
-                out_buf[j] = (tail[j] + x_in[j].astype(jnp.float32)).astype(jnp.bfloat16)
-
-                @pl.when(j > 0)
-                def _():
-                    down_copy(j - 1).start()
-
+            for b in range(2):
+                x_copy(blocks - 2 + b).start()
+
+            def step(j, carry):
+                pass_on(j)
                 return carry
 
-            lax.fori_loop(0, pairs, pass_step, 0)
-            down_copy(pairs - 1).start()
+            lax.fori_loop(0, AHEAD, step, 0)
 
     @pl.when(is_back)
     def _():
@@ -321,18 +348,15 @@
         twin_copy.wait_recv()
 
         def rows_step(j, carry):
-            for b in range(2):
-                for layer in range(2):
-                    z_copy(2 * j + b, layer).wait_recv()
-
-                    @pl.when(odd == 0)
-                    def _():
-                        relay(2 * j + b, layer).start()
-
+            z_both(j).wait_recv()
+
+            @pl.when(odd == 0)
+            def _():
+                relay(j).start()
+
+            relay(j).wait_recv()
             for layer in range(2):
                 nearest = twin if layer == 0 else own
-                for b in range(2):
-                    relay(2 * j + b, layer).wait_recv()
                 window = jnp.concatenate(
                     [
                         jnp.concatenate(
@@ -365,11 +389,14 @@
             )
 
         def give_step(j, carry):
-            out_buf[j] = cols(0, j).astype(jnp.bfloat16)
+            total = cols(0, j).astype(jnp.bfloat16)
+            for b in range(2):
+                out_buf[2 * j + b] = total[:, b * n : (b + 1) * n]
 
             @pl.when(j > 0)
             def _():
-                across_copy(j - 1).start()
+                for b in range(2):
+                    across_copy(2 * j - 2 + b).start()
 
             return carry
 
@@ -380,7 +407,8 @@
 
             @pl.when(j == 0)
             def _():
-                across_copy(pairs - 1).start()
+                for b in range(2):
+                    across_copy(blocks - 2 + b).start()
 
             return carry
 
@@ -389,16 +417,28 @@
     weight_sum = weights_ref[0]
     for a in range(1, slices):
         weight_sum = weight_sum + weights_ref[a]
+    share = 1.0 / jnp.full((8, n), weight_sum, jnp.float32)[0:1]
 
     def final_step(j, carry):
-        across_copy(j).wait_recv()
+        @pl.when(is_front & (odd == 1) & (j < pairs - AHEAD))
+        def _():
+            pass_on(j + AHEAD)
+
+        @pl.when(is_front & (odd == 1) & (j == pairs - AHEAD))
+        def _():
+            down_copy(blocks - 1).start()
 
         @pl.when(is_front & (odd == 0))
         def _():
-            x_copy(j).wait_recv()
-            local[j] = local[j] + x_in[j].astype(jnp.float32)
-
-        c, s = cos_sin(local[j] + in_buf[j].astype(jnp.float32))
+            for b in range(2):
+                x_copy(2 * j + b).wait_recv()
+                part = slice(b * n, (b + 1) * n)
+                local[j, :, part] = local[j, :, part] + x_in[2 * j + b].astype(jnp.float32)
+
+        for b in range(2):
+            across_copy(2 * j + b).wait_recv()
+        arrived = jnp.concatenate([in_buf[2 * j + b].astype(jnp.float32) for b in range(2)], 1)
+        c, s = cos_sin(local[j] + arrived)
         field = jnp.concatenate([c, s], 0).astype(jnp.bfloat16)
         sums = [jnp.zeros((n, n), jnp.float32) for _ in range(2)]
         for a in range(slices):
@@ -424,35 +464,28 @@
         for b in range(2):
             lit = valid_ref[0, 2 * j + b].astype(jnp.float32)
             out_ref[0, 0, :, pl.ds(pl.multiple_of((2 * j + b) * n, n), n)] = (
-                sums[b] / weight_sum * lit
+                sums[b] * (share * lit)
             ).astype(jnp.bfloat16)
         return carry
 
     lax.fori_loop(0, pairs, final_step, 0, unroll=2)
 
-    for k in range(blocks):
-        z_copy(k).wait_send()
+    z_all.wait_send()
+    far_copy.wait_send()
+    twin_copy.wait_send()
+    out_all.wait_send()
 
     @pl.when(odd == 1)
     def _():
-        for k in range(blocks):
-            f_copy(k).wait_send()
-
-    far_copy().wait_send()
-    twin_copy.wait_send()
-    for j in range(pairs):
-        across_copy(j).wait_send()
+        f_all.wait_send()
 
     @pl.when(is_front)
     def _():
-        for j in range(pairs):
-            x_copy(j).wait_send()
+        x_all.wait_send()
 
     @pl.when(is_back & (odd == 0))
     def _():
-        for k in range(blocks):
-            for layer in range(2):
-                relay(k, layer).wait_send()
+        r_all.wait_send()
 
 
 def solution(mesh):
@@ -466,16 +499,19 @@
         fr, fi = base_tables(n)
         right = jnp.asarray(np.block([[fr.T, fi.T], [-fi.T, fr.T]])).astype(jnp.bfloat16)
         vmem = pl.BlockSpec(memory_space=pltpu.VMEM)
-        smem = pl.BlockSpec(memory_space=pltpu.SMEM)
         hbm = pl.BlockSpec(memory_space=pl.ANY)
         dma = pltpu.SemaphoreType.DMA
         half, full = jnp.bfloat16, jnp.float32
         return pl.pallas_call(
             functools.partial(kernel, tiles, n, blocks, slices),
             out_shape=pltpu.VMEM((1, 1, n, cols), half),
-            in_specs=[hbm, smem, smem, smem, smem, hbm, hbm, hbm],
+            in_specs=[hbm] * 7,
             out_specs=vmem,
             scratch_shapes=[
+                pltpu.SMEM((4, 2, 4), jnp.int32),
+                pltpu.SMEM((1, blocks), jnp.int32),
+                pltpu.SMEM((slices,), full),
+                pltpu.SMEM((slices,), full),
                 pltpu.VMEM((blocks, n, n), half),
                 pltpu.VMEM((blocks, n, n), half),
                 pltpu.VMEM((2, blocks, n, n), half),
@@ -486,29 +522,25 @@
                 pltpu.VMEM((4, 3 * n, 2 * n), half),
                 pltpu.VMEM((2, 2 * n, (REACH + 1) * n), half),
                 pltpu.VMEM((2, 6 * n, 2 * n), half),
-                pltpu.VMEM((pairs, n, 2 * n), half),
-                pltpu.VMEM((pairs, n, 2 * n), half),
+                pltpu.VMEM((blocks, n, n), half),
+                pltpu.VMEM((blocks, n, n), half),
                 pltpu.VMEM((pairs, n, 2 * n), full),
-                pltpu.VMEM((pairs, n, 2 * n), half),
-                pltpu.VMEM((pairs, n, 2 * n), half),
+                pltpu.VMEM((blocks, n, n), half),
+                pltpu.VMEM((blocks, n, n), half),
                 pltpu.VMEM((pairs, n, 2 * n), full),
                 pltpu.VMEM((2 * slices * n, 2 * n), half),
                 pltpu.VMEM((pairs, slices, 8, 2 * n), full),
                 pltpu.VMEM((pairs, slices, 8, 2 * n), full),
-                pltpu.VMEM((n, n), full),
-                pltpu.VMEM((n, n), full),
+                pltpu.VMEM((2, n, n), full),
                 pltpu.VMEM((2 * n, 2 * n), half),
-                dma((blocks,)), dma((3,)),
-                dma((blocks,)), dma((2, blocks)),
-                dma((blocks,)), dma((2, blocks)), dma((2, blocks)),
-                dma, dma((2,)),
-                dma, dma,
-                dma((pairs,)), dma((pairs,)),
-                dma((pairs,)), dma((pairs,)),
+                dma, dma((6,)),
+                dma, dma((pairs,)), dma, dma, dma((pairs,)),
+                dma, dma, dma, dma,
+                dma, dma((blocks,)), dma, dma((blocks,)),
                 pltpu.SemaphoreType.REGULAR,
             ],
             compiler_params=pltpu.CompilerParams(collective_id=0, has_side_effects=True),
-        )(layers, jnp.transpose(offsets, (0, 2, 1)), subap_valid, defocus, weights, jnp.asarray(fr), jnp.asarray(fi), right)
+        )(layers, jnp.transpose(offsets, (0, 2, 1)), subap_valid, defocus, weights, jnp.asarray(np.stack([fr, fi])), right)
 
     placed = (P("dir", "tile", None), P(), P("tile", None), P(), P())
     return jax.shard_map(

time: 35.1 us -> 33 us (0.940)
  the two profiles are of different devices: /device:TPU:31 before, /device:TPU:2 now
where the time goes in v3:
time: 33 us; the launch traced here: 32.9 us
  Pallas kernels  32.1 us (97%)
  local copies, waits for them, and re-layouts  0.8 us (2%)
    pallas_call x1, Pallas kernels, shards(): pl.pallas_call(functools.partial(kernel, tiles, n, blocks, slices), out_s...  32.1 us
    unnamed x1, local copies, waits for them, and re-layouts  0.8 us

profile of v3, /device:TPU:2, one launch (start us, length us, event | category | flops | bytes accessed | tf_op | source)
XLA Modules:
  0.0 32.9 jit_solution(15283746611461740824)
XLA Ops:
  0.0 32.1 %shard_map.73 = bf16[1,1,128,2048]{3,2,1,0:T(8,128)(2,1)S(1)} custom-call(bf16[1,128,2048]{2,1,0:T(8,128)(2,1)} %x_ref.1, s32[4,2,4]{2,1,0:T(2,128)} %bitcast.1, s32[1,16]{1,0:T(1,128)} %valid_hbm.1, f32[3]{0:T(128)} %defocus_hbm.1, f32[3]{0:T(128)} %weights_hbm.1, f32[2,128,128]{2,1,0:T(8,128)} %constant.5.clone.base_ref, bf16[256,256]{1,0:T(8,128)(2,1)} %constant.8.right_ref), custom_call_target="tpu_custom_call" | custom-call | tf_op jit(solution)/shard_map/pallas_call | solution.py:505
  32.1 0.8 %copy.9 = bf16[1,1,128,2048]{3,2,1,0:T(8,128)(2,1)} copy(bf16[1,1,128,2048]{3,2,1,0:T(8,128)(2,1)S(1)} %shard_map.73) | data formatting | bytes 1048576

commit v4 on v3

--- a/solution.py
+++ b/solution.py
@@ -12,8 +12,9 @@
 OVER = 2
 QUANT = 4
 REACH = 2
-GROUP = 4
-AHEAD = 8
+GROUP = 8
+BATCH = 4
+LEAD = 2
 MESH = pl.DeviceIdType.MESH
 SIN = (3.141582022082025, -5.167142794167084, 2.541899009948703, -0.5546361567315732)
 COS = (0.999999953466345, -4.934792858633932, 4.058411913339297, -1.3318801559459539, 0.21969678799073292)
@@ -55,9 +56,9 @@
     x_ref, off_hbm, valid_hbm, defocus_hbm, weights_hbm, base_ref, right_ref,
     out_ref,
     off_ref, valid_ref, defocus_ref, weights_ref, own, twin, far, halo, mixed, moved, front_mix, front_slide, back_mix, back_slide,
-    x_buf, x_in, tail, out_buf, in_buf, local, left, col_cos, col_sin, base_tab, right_tab,
+    x_buf, x_in, tail, out_buf, in_buf, local, left, col_cos, col_sin, base_tab, right_tab, field_buf,
     load_sem, table_sem, z_send, z_recv, f_send, r_send, h_recv, y_send, y_recv, t_send, t_recv,
-    x_send, x_recv, o_send, o_recv, ready,
+    x_send, x_recv, o_send, o_recv, ready, go,
 ):
     tile = lax.axis_index("tile")
     place = lax.axis_index("dir")
@@ -80,21 +81,18 @@
 
     first, last = tile < 2, tile >= tiles - 2
 
+    @pl.when(is_back)
+    def _():
+        greet((above, back))
+
     @pl.when(jnp.logical_not(last))
     def _():
-        greet((above, front + core))
-
-        @pl.when(is_back)
-        def _():
-            greet((above, front))
-
-    @pl.when(first)
+        greet((above, front))
+
+    @pl.when(first & is_front)
     def _():
         greet((below, back))
-
-        @pl.when(is_front)
-        def _():
-            greet((below, front))
+        greet((below, front))
 
     @pl.when(is_front)
     def _():
@@ -133,9 +131,10 @@
     def pair_of(k):
         return pl.ds(2 * k, 2)
 
-    def z_copy(k):
+    def z_copy(k, layer=core):
         return copy(
-            own.at[pair_of(k)], halo.at[core, 1, pair_of(k)], z_send, z_recv.at[k], (below, back)
+            own.at[pair_of(k)], halo.at[layer, 1, pair_of(k)], z_send, z_recv.at[layer, k],
+            (below, back),
         )
 
     def f_copy(k):
@@ -143,16 +142,17 @@
             own.at[pair_of(k)], halo.at[core, 0, pair_of(k)], f_send, h_recv.at[k], (mate, back)
         )
 
-    def relay(k):
+    def relay(k, layer):
         return copy(
-            halo.at[:, 1, pair_of(k)], halo.at[:, 0, pair_of(k)], r_send, h_recv.at[k], (mate, back)
+            halo.at[layer, 1, pair_of(k)], halo.at[layer, 0, pair_of(k)], r_send, h_recv.at[k],
+            (mate, back),
         )
 
-    def z_both(k):
-        part = halo.at[:, 1, pair_of(k)]
-        return copy(part, part, r_send, z_recv.at[k], (mate, back))
-
-    z_all = copy(own, halo.at[core, 1], z_send, z_recv.at[0], (below, back))
+    def h_both(k):
+        part = halo.at[:, 0, pair_of(k)]
+        return copy(part, part, r_send, h_recv.at[k], (mate, back))
+
+    z_all = copy(own, halo.at[core, 1], z_send, z_recv.at[0, 0], (below, back))
     f_all = copy(own, halo.at[core, 0], f_send, h_recv.at[0], (mate, back))
     r_all = copy(halo.at[:, 1], halo.at[:, 0], r_send, h_recv.at[0], (mate, back))
     far_copy = copy(own, far.at[core], y_send, y_recv, (tile, far_front))
@@ -164,7 +164,7 @@
         return copy(x_buf.at[j], x_in.at[j], x_send, x_recv.at[j], (mate, front))
 
     def down_copy(j):
-        return copy(out_buf.at[j], in_buf.at[j], o_send, o_recv.at[j], (below, front))
+        return copy(out_buf.at[j], in_buf.at[j], o_send, o_recv.at[lax.div(j, 2)], (below, front))
 
     def pass_on(j):
         for b in range(2):
@@ -179,38 +179,38 @@
                 down_copy(k - 1).start()
 
     def across_copy(j):
-        return copy(out_buf.at[j], in_buf.at[j], o_send, o_recv.at[j], (tile, far_back))
+        return copy(
+            out_buf.at[j], in_buf.at[j], o_send, o_recv.at[lax.div(j, 2)], (tile, far_back)
+        )
+
+    def await_in(j):
+        part = pair_of(j)
+        copy(out_buf.at[part], in_buf.at[part], o_send, o_recv.at[j], (tile, far_back)).wait_recv()
 
     x_all = copy(x_buf, x_in, x_send, x_recv.at[0], (mate, front))
     out_all = copy(out_buf, in_buf, o_send, o_recv.at[0], (tile, far_back))
 
-    downward = jnp.where(is_front, 2, 1)
-    upward = jnp.where(is_front, 1, 2)
+    held = first & is_front
     pl.semaphore_wait(
         barrier,
-        5 + jnp.where(is_front, odd, 0) - jnp.where(first, downward, 0) + jnp.where(last, upward, 0),
+        5 + jnp.where(is_front, odd, 0) - jnp.where(held, 2, 0) + jnp.where(last, 1, 0),
     )
 
     @pl.when(last)
     def _():
-        def answer(device):
-            pl.semaphore_signal(ready, inc=1, device_id=device, device_id_type=MESH)
-
-        answer((above, front))
-
-        @pl.when(is_back)
-        def _():
-            answer((above, back))
+        pl.semaphore_signal(
+            ready.at[core], inc=1, device_id=(above, front), device_id_type=MESH
+        )
 
     pltpu.make_async_copy(twin, own, load_sem).wait()
-    for k in range(pairs):
-
-        @pl.when(jnp.logical_not(first))
-        def _():
+    @pl.when(jnp.logical_not(held))
+    def _():
+        for k in range(pairs):
             z_copy(k).start()
 
-        @pl.when(odd == 1)
-        def _():
+    @pl.when(odd == 1)
+    def _():
+        for k in range(pairs):
             f_copy(k).start()
 
     far_copy.start()
@@ -223,9 +223,13 @@
     p = (first_row + row_at - (tiles * n - 1) / 2.0) / n
     col_at = lax.broadcasted_iota(jnp.int32, (8, blocks * n), 1).astype(jnp.float32)
     q = (col_at - (blocks * n - 1) / 2.0) / n
+    weight_sum = weights_ref[0]
+    for a in range(1, slices):
+        weight_sum = weight_sum + weights_ref[a]
     for a in range(slices):
         row_cos, row_sin = cos_sin(defocus_ref[a] * (p * p))
-        row_cos, row_sin = row_cos[0:1], row_sin[0:1]
+        share = jnp.sqrt(jnp.full((8, n), weights_ref[a], jnp.float32) / weight_sum)
+        row_cos, row_sin = (row_cos * share)[0:1], (row_sin * share)[0:1]
         real = base_tab[0] * row_cos - base_tab[1] * row_sin
         imag = base_tab[0] * row_sin + base_tab[1] * row_cos
         left[2 * a * n : (2 * a + 1) * n, 0:n] = real.astype(jnp.bfloat16)
@@ -237,9 +241,9 @@
             col_cos[j, a] = c[:, j * 2 * n : (j + 1) * 2 * n]
             col_sin[j, a] = s[:, j * 2 * n : (j + 1) * 2 * n]
 
-    @pl.when(first)
-    def _():
-        pl.semaphore_wait(ready, downward)
+    @pl.when(held)
+    def _():
+        pl.semaphore_wait(ready.at[1], 1)
         for k in range(pairs):
             z_copy(k).start()
 
@@ -288,8 +292,26 @@
         twin_copy.wait_recv()
         shift(1, lambda b: twin[b])
         far_both.wait_recv()
-        for layer in range(2):
-            shift(2 + layer, lambda b: far[layer, b])
+        groups = pairs // GROUP
+
+        def far_step(i, carry):
+            side, g = lax.div(i, groups), lax.rem(i, groups)
+            begin = jnp.where(side == 0, plans[2][4], plans[3][4])
+            rows = []
+            for j in range(GROUP):
+                at = begin + 2 * (g * GROUP + j)
+                rows.append(
+                    jnp.concatenate([far[side, (at + b) & (blocks - 1)] for b in range(3)], 1)
+                )
+            total = jnp.dot(
+                jnp.concatenate(rows, 0), front_slide[2 + side], preferred_element_type=jnp.float32
+            ).astype(jnp.bfloat16)
+            place_at = pl.ds(pl.multiple_of((2 + side) * n, n), n)
+            for j in range(GROUP):
+                mixed[g * GROUP + j, place_at, :] = total[j * n : (j + 1) * n]
+            return carry
+
+        lax.fori_loop(0, 2 * groups, far_step, 0)
 
         def give_step(j, carry):
             total = jnp.dot(front_mix[...], mixed[j], preferred_element_type=jnp.float32)
@@ -300,37 +322,46 @@
                 x_buf[2 * j + b] = total[n : 2 * n, part].astype(jnp.bfloat16)
                 out_buf[2 * j + b] = total[2 * n :, part].astype(jnp.bfloat16)
 
-            @pl.when((j > 0) & (odd == 0))
-            def _():
-                for b in range(2):
-                    down_copy(2 * j - 2 + b).start()
-
-            @pl.when((j > 0) & (odd == 1))
-            def _():
-                for b in range(2):
-                    x_copy(2 * j - 2 + b).start()
-
-            return carry
-
-        lax.fori_loop(0, pairs, give_step, 0, unroll=2)
-
-        @pl.when(odd == 0)
+            return carry
+
+        @pl.when(first)
         def _():
-            for b in range(2):
-                down_copy(blocks - 2 + b).start()
+            pl.semaphore_wait(ready.at[0], 1)
+
+        for half in range(2):
+            lax.fori_loop(half * pairs // 2, (half + 1) * pairs // 2, give_step, 0, unroll=2)
+            ready_blocks = range(half * blocks // 2, (half + 1) * blocks // 2)
+
+            @pl.when(odd == 0)
+            def _():
+                for k in ready_blocks:
+                    down_copy(k).start()
+
+            @pl.when((odd == 0) & jnp.logical_not(last))
+            def _():
+                if half == 0:
+                    pl.semaphore_wait(go, 1)
+                for k in ready_blocks:
+                    x_copy(k).start()
+
+            @pl.when(odd == 1)
+            def _():
+                for k in ready_blocks:
+                    x_copy(k).start()
+
+        @pl.when((odd == 0) & last)
+        def _():
+            pl.semaphore_wait(go, 1)
             for k in range(blocks):
                 x_copy(k).start()
 
         @pl.when(odd == 1)
         def _():
-            for b in range(2):
-                x_copy(blocks - 2 + b).start()
-
             def step(j, carry):
                 pass_on(j)
                 return carry
 
-            lax.fori_loop(0, AHEAD, step, 0)
+            lax.fori_loop(0, pairs, step, 0)
 
     @pl.when(is_back)
     def _():
@@ -347,14 +378,29 @@
                 )
         twin_copy.wait_recv()
 
+        lead = jnp.where(last & (odd == 0), LEAD, 0)
+
+        def take(k, layer):
+            z_copy(k, layer).wait_recv()
+
+            @pl.when(odd == 0)
+            def _():
+                relay(k, layer).start()
+
+        def lead_step(k, carry):
+            take(k, 1)
+            return carry
+
+        lax.fori_loop(0, lead, lead_step, 0)
+
         def rows_step(j, carry):
-            z_both(j).wait_recv()
-
-            @pl.when(odd == 0)
-            def _():
-                relay(j).start()
-
-            relay(j).wait_recv()
+            take(j, 0)
+
+            @pl.when(j + lead < pairs)
+            def _():
+                take(j + lead, 1)
+
+            h_both(j).wait_recv()
             for layer in range(2):
                 nearest = twin if layer == 0 else own
                 window = jnp.concatenate(
@@ -378,97 +424,120 @@
 
         lax.fori_loop(0, pairs, rows_step, 0)
 
-        def cols(index, j):
-            parts = []
-            for layer in range(2):
-                begin = plans[index][layer][4] + 2 * j
-                for b in range(3):
-                    parts.append(moved[layer, index, (begin + b) & (blocks - 1)])
+        @pl.when(odd == 0)
+        def _():
+            pl.semaphore_signal(go, inc=1, device_id=(tile, partner), device_id_type=MESH)
+
+        def cols(index, g):
+            rows = []
+            for j in range(BATCH):
+                parts = []
+                for layer in range(2):
+                    begin = plans[index][layer][4] + 2 * (g * BATCH + j)
+                    for b in range(3):
+                        parts.append(moved[layer, index, (begin + b) & (blocks - 1)])
+                rows.append(jnp.concatenate(parts, 1))
             return jnp.dot(
-                jnp.concatenate(parts, 1), back_slide[index], preferred_element_type=jnp.float32
+                jnp.concatenate(rows, 0), back_slide[index], preferred_element_type=jnp.float32
             )
 
-        def give_step(j, carry):
-            total = cols(0, j).astype(jnp.bfloat16)
-            for b in range(2):
-                out_buf[2 * j + b] = total[:, b * n : (b + 1) * n]
-
-            @pl.when(j > 0)
-            def _():
+        def give_step(g, carry):
+            total = cols(0, g).astype(jnp.bfloat16)
+            for j in range(BATCH):
                 for b in range(2):
-                    across_copy(2 * j - 2 + b).start()
-
-            return carry
-
-        lax.fori_loop(0, pairs, give_step, 0, unroll=2)
-
-        def keep_step(j, carry):
-            local[j] = cols(1, j)
-
-            @pl.when(j == 0)
-            def _():
-                for b in range(2):
-                    across_copy(blocks - 2 + b).start()
-
-            return carry
-
-        lax.fori_loop(0, pairs, keep_step, 0, unroll=2)
-
-    weight_sum = weights_ref[0]
-    for a in range(1, slices):
-        weight_sum = weight_sum + weights_ref[a]
-    share = 1.0 / jnp.full((8, n), weight_sum, jnp.float32)[0:1]
-
-    def final_step(j, carry):
-        @pl.when(is_front & (odd == 1) & (j < pairs - AHEAD))
-        def _():
-            pass_on(j + AHEAD)
-
-        @pl.when(is_front & (odd == 1) & (j == pairs - AHEAD))
-        def _():
-            down_copy(blocks - 1).start()
-
-        @pl.when(is_front & (odd == 0))
-        def _():
-            for b in range(2):
-                x_copy(2 * j + b).wait_recv()
-                part = slice(b * n, (b + 1) * n)
-                local[j, :, part] = local[j, :, part] + x_in[2 * j + b].astype(jnp.float32)
-
-        for b in range(2):
-            across_copy(2 * j + b).wait_recv()
+                    out_buf[2 * (g * BATCH + j) + b] = total[j * n : (j + 1) * n, b * n : (b + 1) * n]
+
+            @pl.when(g > 0)
+            def _():
+                for k in range(2 * BATCH):
+                    across_copy(2 * (g - 1) * BATCH + k).start()
+
+            return carry
+
+        lax.fori_loop(0, pairs // BATCH, give_step, 0)
+
+        def keep_step(g, carry):
+            total = cols(1, g)
+            for j in range(BATCH):
+                local[g * BATCH + j] = total[j * n : (j + 1) * n]
+
+            @pl.when(g == 0)
+            def _():
+                for k in range(2 * BATCH):
+                    across_copy(blocks - 2 * BATCH + k).start()
+
+            return carry
+
+        lax.fori_loop(0, pairs // BATCH, keep_step, 0)
+
+    def field_of(j):
         arrived = jnp.concatenate([in_buf[2 * j + b].astype(jnp.float32) for b in range(2)], 1)
         c, s = cos_sin(local[j] + arrived)
-        field = jnp.concatenate([c, s], 0).astype(jnp.bfloat16)
-        sums = [jnp.zeros((n, n), jnp.float32) for _ in range(2)]
+        return jnp.concatenate([c, s], 0).astype(jnp.bfloat16)
+
+    def spots(j, field):
+        focal = jnp.dot(left[...], field, preferred_element_type=jnp.float32)
+        fields = []
         for a in range(slices):
-            focal = jnp.dot(
-                left[2 * a * n : (2 * a + 2) * n, :], field, preferred_element_type=jnp.float32
-            )
-            real, imag = focal[:n], focal[n:]
+            real, imag = focal[2 * a * n : (2 * a + 1) * n], focal[(2 * a + 1) * n : (2 * a + 2) * n]
             c, s = col_cos[j, a][0:1], col_sin[j, a][0:1]
             new_real = (real * c - imag * s).astype(jnp.bfloat16)
             new_imag = (real * s + imag * c).astype(jnp.bfloat16)
-            both = jnp.concatenate(
-                [
+            for b in range(2):
+                fields.append(
                     jnp.concatenate([new_real[:, b * n : (b + 1) * n], new_imag[:, b * n : (b + 1) * n]], 1)
-                    for b in range(2)
-                ],
-                0,
+                )
+        spot = jnp.dot(jnp.concatenate(fields, 0), right_tab[...], preferred_element_type=jnp.float32)
+        power = spot * spot
+        for b in range(2):
+            total = 0.0
+            for a in range(slices):
+                piece = power[(2 * a + b) * n : (2 * a + b + 1) * n]
+                total = total + (piece[:, :n] + piece[:, n:])
+            lit = valid_ref[0, 2 * j + b].astype(jnp.float32)
+            out_ref[0, 0, :, pl.ds(pl.multiple_of((2 * j + b) * n, n), n)] = (total * lit).astype(
+                jnp.bfloat16
             )
-            spot = jnp.dot(both, right_tab[...], preferred_element_type=jnp.float32)
-            power = spot * spot
-            for b in range(2):
-                piece = power[b * n : (b + 1) * n]
-                sums[b] = sums[b] + weights_ref[a] * (piece[:, :n] + piece[:, n:])
-        for b in range(2):
-            lit = valid_ref[0, 2 * j + b].astype(jnp.float32)
-            out_ref[0, 0, :, pl.ds(pl.multiple_of((2 * j + b) * n, n), n)] = (
-                sums[b] * (share * lit)
-            ).astype(jnp.bfloat16)
-        return carry
-
-    lax.fori_loop(0, pairs, final_step, 0, unroll=2)
+
+    passing = is_front & (odd == 1)
+
+    @pl.when(jnp.logical_not(passing))
+    def _():
+        def final_step(j, carry):
+            @pl.when(is_front)
+            def _():
+                for b in range(2):
+                    x_copy(2 * j + b).wait_recv()
+                    part = slice(b * n, (b + 1) * n)
+                    local[j, :, part] = local[j, :, part] + x_in[2 * j + b].astype(jnp.float32)
+
+            await_in(j)
+            spots(j, field_of(j))
+            return carry
+
+        lax.fori_loop(0, pairs, final_step, 0, unroll=2)
+
+    @pl.when(passing)
+    def _():
+        down_copy(blocks - 1).start()
+        await_in(0)
+        field_buf[0] = field_of(0)
+
+        def final_step(i, carry):
+            j = 2 * i
+            await_in(j + 1)
+            field_buf[1] = field_of(j + 1)
+            spots(j, field_buf[0])
+            await_in(j + 2)
+            field_buf[0] = field_of(j + 2)
+            spots(j + 1, field_buf[1])
+            return carry
+
+        lax.fori_loop(0, pairs // 2 - 1, final_step, 0)
+        await_in(pairs - 1)
+        field_buf[1] = field_of(pairs - 1)
+        spots(pairs - 2, field_buf[0])
+        spots(pairs - 1, field_buf[1])
 
     z_all.wait_send()
     far_copy.wait_send()
@@ -533,10 +602,12 @@
                 pltpu.VMEM((pairs, slices, 8, 2 * n), full),
                 pltpu.VMEM((2, n, n), full),
                 pltpu.VMEM((2 * n, 2 * n), half),
+                pltpu.VMEM((2, 2 * n, 2 * n), half),
                 dma, dma((6,)),
-                dma, dma((pairs,)), dma, dma, dma((pairs,)),
+                dma, dma((2, pairs)), dma, dma, dma((pairs,)),
                 dma, dma, dma, dma,
-                dma, dma((blocks,)), dma, dma((blocks,)),
+                dma, dma((blocks,)), dma, dma((pairs,)),
+                pltpu.SemaphoreType.REGULAR((2,)),
                 pltpu.SemaphoreType.REGULAR,
             ],
             compiler_params=pltpu.CompilerParams(collective_id=0, has_side_effects=True),

time: 33 us -> 31.1 us (0.942)
  Pallas kernels: 32.1 us -> 30.1 us
    pallas_call x1, Pallas kernels: 32.1 us -> 30.1 us  [shards(): pl.pallas_call(functools.partial(kernel, tiles, n, blocks, slices), out_s...]
where the time goes in v4:
time: 31.1 us; the launch traced here: 30.9 us
  Pallas kernels  30.1 us (97%)
  local copies, waits for them, and re-layouts  0.8 us (3%)
    pallas_call x1, Pallas kernels, shards(): pl.pallas_call(functools.partial(kernel, tiles, n, blocks, slices), out_s...  30.1 us
    unnamed x1, local copies, waits for them, and re-layouts  0.8 us

profile of v4, /device:TPU:2, one launch (start us, length us, event | category | flops | bytes accessed | tf_op | source)
XLA Modules:
  0.0 30.9 jit_solution(10046337984401021799)
XLA Ops:
  0.0 30.1 %shard_map.73 = bf16[1,1,128,2048]{3,2,1,0:T(8,128)(2,1)S(1)} custom-call(bf16[1,128,2048]{2,1,0:T(8,128)(2,1)} %x_ref.1, s32[4,2,4]{2,1,0:T(2,128)} %bitcast.1, s32[1,16]{1,0:T(1,128)} %valid_hbm.1, f32[3]{0:T(128)} %defocus_hbm.1, f32[3]{0:T(128)} %weights_hbm.1, f32[2,128,128]{2,1,0:T(8,128)} %constant.5.clone.base_ref, bf16[256,256]{1,0:T(8,128)(2,1)} %constant.8.right_ref), custom_call_target="tpu_custom_call" | custom-call | tf_op jit(solution)/shard_map/pallas_call | solution.py:574
  30.1 0.8 %copy.9 = bf16[1,1,128,2048]{3,2,1,0:T(8,128)(2,1)} copy(bf16[1,1,128,2048]{3,2,1,0:T(8,128)(2,1)S(1)} %shard_map.73) | data formatting | bytes 1048576

commit v5 on v4

--- a/solution.py
+++ b/solution.py
@@ -15,6 +15,8 @@
 GROUP = 8
 BATCH = 4
 LEAD = 2
+PACE = 2
+DETOUR = 1
 MESH = pl.DeviceIdType.MESH
 SIN = (3.141582022082025, -5.167142794167084, 2.541899009948703, -0.5546361567315732)
 COS = (0.999999953466345, -4.934792858633932, 4.058411913339297, -1.3318801559459539, 0.21969678799073292)
@@ -55,10 +57,10 @@
     tiles, n, blocks, slices,
     x_ref, off_hbm, valid_hbm, defocus_hbm, weights_hbm, base_ref, right_ref,
     out_ref,
-    off_ref, valid_ref, defocus_ref, weights_ref, own, twin, far, halo, mixed, moved, front_mix, front_slide, back_mix, back_slide,
+    off_ref, valid_ref, defocus_ref, weights_ref, own, twin, far, halo, via, mixed, moved, front_mix, front_slide, back_mix, back_slide,
     x_buf, x_in, tail, out_buf, in_buf, local, left, col_cos, col_sin, base_tab, right_tab, field_buf,
     load_sem, table_sem, z_send, z_recv, f_send, r_send, h_recv, y_send, y_recv, t_send, t_recv,
-    x_send, x_recv, o_send, o_recv, ready, go,
+    x_send, x_recv, o_send, o_recv, v_send, v_recv, ready,
 ):
     tile = lax.axis_index("tile")
     place = lax.axis_index("dir")
@@ -100,9 +102,7 @@
 
     @pl.when(is_back)
     def _():
-        @pl.when(odd == 0)
-        def _():
-            greet((mate, front))
+        greet((mate, front))
 
     greet((mate, front + core))
     greet((tile, far_front + core))
@@ -152,9 +152,25 @@
         part = halo.at[:, 0, pair_of(k)]
         return copy(part, part, r_send, h_recv.at[k], (mate, back))
 
+    straight = pairs - DETOUR
+    rest = pl.ds(2 * straight, 2 * DETOUR)
+
+    def detour(layer=core):
+        return copy(own.at[rest], via.at[layer], v_send, v_recv, (mate, back))
+
+    detour_both = copy(via, via, v_send, v_recv, (mate, back))
+
+    def onward(k):
+        part = pl.ds(2 * (k - straight), 2)
+        return copy(
+            via.at[:, part], halo.at[:, 0, pair_of(k)], r_send, h_recv.at[k], (below, back)
+        )
+
     z_all = copy(own, halo.at[core, 1], z_send, z_recv.at[0, 0], (below, back))
     f_all = copy(own, halo.at[core, 0], f_send, h_recv.at[0], (mate, back))
-    r_all = copy(halo.at[:, 1], halo.at[:, 0], r_send, h_recv.at[0], (mate, back))
+    before = pl.ds(0, 2 * straight)
+    r_all = copy(halo.at[:, 1, before], halo.at[:, 0, before], r_send, h_recv.at[0], (mate, back))
+    onward_all = copy(via, via, r_send, h_recv.at[0], (below, back))
     far_copy = copy(own, far.at[core], y_send, y_recv, (tile, far_front))
     far_both = copy(far, far, y_send, y_recv, (tile, far_front))
 
@@ -193,7 +209,7 @@
     held = first & is_front
     pl.semaphore_wait(
         barrier,
-        5 + jnp.where(is_front, odd, 0) - jnp.where(held, 2, 0) + jnp.where(last, 1, 0),
+        5 + jnp.where(is_front, 1, 0) - jnp.where(held, 2, 0) + jnp.where(last, 1, 0),
     )
 
     @pl.when(last)
@@ -203,6 +219,10 @@
         )
 
     pltpu.make_async_copy(twin, own, load_sem).wait()
+    @pl.when(odd == 0)
+    def _():
+        detour().start()
+
     @pl.when(jnp.logical_not(held))
     def _():
         for k in range(pairs):
@@ -292,76 +312,65 @@
         twin_copy.wait_recv()
         shift(1, lambda b: twin[b])
         far_both.wait_recv()
-        groups = pairs // GROUP
-
-        def far_step(i, carry):
-            side, g = lax.div(i, groups), lax.rem(i, groups)
-            begin = jnp.where(side == 0, plans[2][4], plans[3][4])
-            rows = []
-            for j in range(GROUP):
-                at = begin + 2 * (g * GROUP + j)
-                rows.append(
-                    jnp.concatenate([far[side, (at + b) & (blocks - 1)] for b in range(3)], 1)
-                )
-            total = jnp.dot(
-                jnp.concatenate(rows, 0), front_slide[2 + side], preferred_element_type=jnp.float32
-            ).astype(jnp.bfloat16)
-            place_at = pl.ds(pl.multiple_of((2 + side) * n, n), n)
-            for j in range(GROUP):
-                mixed[g * GROUP + j, place_at, :] = total[j * n : (j + 1) * n]
-            return carry
-
-        lax.fori_loop(0, 2 * groups, far_step, 0)
-
-        def give_step(j, carry):
-            total = jnp.dot(front_mix[...], mixed[j], preferred_element_type=jnp.float32)
-            local[j] = total[:n]
-            tail[j] = total[2 * n :]
-            for b in range(2):
-                part = slice(b * n, (b + 1) * n)
-                x_buf[2 * j + b] = total[n : 2 * n, part].astype(jnp.bfloat16)
-                out_buf[2 * j + b] = total[2 * n :, part].astype(jnp.bfloat16)
-
-            return carry
-
         @pl.when(first)
         def _():
             pl.semaphore_wait(ready.at[0], 1)
 
-        for half in range(2):
-            lax.fori_loop(half * pairs // 2, (half + 1) * pairs // 2, give_step, 0, unroll=2)
-            ready_blocks = range(half * blocks // 2, (half + 1) * blocks // 2)
+        def send_pair(j):
+            for b in range(2):
+                x_copy(2 * j + b).start()
 
             @pl.when(odd == 0)
             def _():
-                for k in ready_blocks:
-                    down_copy(k).start()
-
-            @pl.when((odd == 0) & jnp.logical_not(last))
-            def _():
-                if half == 0:
-                    pl.semaphore_wait(go, 1)
-                for k in ready_blocks:
-                    x_copy(k).start()
-
-            @pl.when(odd == 1)
-            def _():
-                for k in ready_blocks:
-                    x_copy(k).start()
-
-        @pl.when((odd == 0) & last)
-        def _():
-            pl.semaphore_wait(go, 1)
-            for k in range(blocks):
-                x_copy(k).start()
+                for b in range(2):
+                    down_copy(2 * j + b).start()
+
+        def give_step(g, carry):
+            for side in range(2):
+                begin = plans[2 + side][4] + 2 * PACE * g
+                rows = []
+                for j in range(PACE):
+                    rows.append(
+                        jnp.concatenate(
+                            [far[side, (begin + 2 * j + b) & (blocks - 1)] for b in range(3)], 1
+                        )
+                    )
+                total = jnp.dot(
+                    jnp.concatenate(rows, 0), front_slide[2 + side], preferred_element_type=jnp.float32
+                ).astype(jnp.bfloat16)
+                for j in range(PACE):
+                    mixed[g * PACE + j, (2 + side) * n : (3 + side) * n, :] = total[j * n : (j + 1) * n]
+            for i in range(PACE):
+                j = g * PACE + i
+                total = jnp.dot(front_mix[...], mixed[j], preferred_element_type=jnp.float32)
+                local[j] = total[:n]
+                tail[j] = total[2 * n :]
+                for b in range(2):
+                    part = slice(b * n, (b + 1) * n)
+                    x_buf[2 * j + b] = total[n : 2 * n, part].astype(jnp.bfloat16)
+                    out_buf[2 * j + b] = total[2 * n :, part].astype(jnp.bfloat16)
+            @pl.when(g > 0)
+            def _():
+                send_pair(g * PACE - 1)
+
+            for j in range(PACE - 1):
+                send_pair(g * PACE + j)
+            return carry
+
+        lax.fori_loop(0, pairs // PACE, give_step, 0)
+
 
         @pl.when(odd == 1)
         def _():
+            pass_on(0)
+            for b in range(2):
+                x_copy(blocks - 2 + b).start()
+
             def step(j, carry):
                 pass_on(j)
                 return carry
 
-            lax.fori_loop(0, pairs, step, 0)
+            lax.fori_loop(1, pairs, step, 0)
 
     @pl.when(is_back)
     def _():
@@ -383,7 +392,7 @@
         def take(k, layer):
             z_copy(k, layer).wait_recv()
 
-            @pl.when(odd == 0)
+            @pl.when((odd == 0) & (k < straight))
             def _():
                 relay(k, layer).start()
 
@@ -392,6 +401,12 @@
             return carry
 
         lax.fori_loop(0, lead, lead_step, 0)
+
+        @pl.when(odd == 1)
+        def _():
+            detour_both.wait_recv()
+            for k in range(straight, pairs):
+                onward(k).start()
 
         def rows_step(j, carry):
             take(j, 0)
@@ -423,10 +438,6 @@
             return carry
 
         lax.fori_loop(0, pairs, rows_step, 0)
-
-        @pl.when(odd == 0)
-        def _():
-            pl.semaphore_signal(go, inc=1, device_id=(tile, partner), device_id_type=MESH)
 
         def cols(index, g):
             rows = []
@@ -511,6 +522,12 @@
                     part = slice(b * n, (b + 1) * n)
                     local[j, :, part] = local[j, :, part] + x_in[2 * j + b].astype(jnp.float32)
 
+                @pl.when(j == 0)
+                def _():
+                    for b in range(2):
+                        x_copy(blocks - 2 + b).start()
+                        down_copy(blocks - 2 + b).start()
+
             await_in(j)
             spots(j, field_of(j))
             return carry
@@ -552,9 +569,17 @@
     def _():
         x_all.wait_send()
 
+    @pl.when(odd == 0)
+    def _():
+        detour().wait_send()
+
     @pl.when(is_back & (odd == 0))
     def _():
         r_all.wait_send()
+
+    @pl.when(is_back & (odd == 1))
+    def _():
+        onward_all.wait_send()
 
 
 def solution(mesh):
@@ -585,6 +610,7 @@
                 pltpu.VMEM((blocks, n, n), half),
                 pltpu.VMEM((2, blocks, n, n), half),
                 pltpu.VMEM((2, REACH, blocks, n, n), half),
+                pltpu.VMEM((2, 2 * DETOUR, n, n), half),
                 pltpu.VMEM((pairs, 4 * n, 2 * n), half),
                 pltpu.VMEM((2, 2, blocks, n, n), half),
                 pltpu.VMEM(((REACH + 1) * n, 4 * n), half),
@@ -606,9 +632,8 @@
                 dma, dma((6,)),
                 dma, dma((2, pairs)), dma, dma, dma((pairs,)),
                 dma, dma, dma, dma,
-                dma, dma((blocks,)), dma, dma((pairs,)),
+                dma, dma((blocks,)), dma, dma((pairs,)), dma, dma,
                 pltpu.SemaphoreType.REGULAR((2,)),
-                pltpu.SemaphoreType.REGULAR,
             ],
             compiler_params=pltpu.CompilerParams(collective_id=0, has_side_effects=True),
         )(layers, jnp.transpose(offsets, (0, 2, 1)), subap_valid, defocus, weights, jnp.asarray(np.stack([fr, fi])), right)

time: 31.1 us -> 29.9 us (0.961)
  Pallas kernels: 30.1 us -> 29 us
    pallas_call x1, Pallas kernels: 30.1 us -> 29 us  [shards(): pl.pallas_call(functools.partial(kernel, tiles, n, blocks, slices), out_s...]
where the time goes in v5:
time: 29.9 us; the launch traced here: 29.8 us
  Pallas kernels  29 us (97%)
  local copies, waits for them, and re-layouts  0.8 us (3%)
    pallas_call x1, Pallas kernels, shards(): pl.pallas_call(functools.partial(kernel, tiles, n, blocks, slices), out_s...  29 us
    unnamed x1, local copies, waits for them, and re-layouts  0.8 us

profile of v5, /device:TPU:2, one launch (start us, length us, event | category | flops | bytes accessed | tf_op | source)
XLA Modules:
  0.0 29.8 jit_solution(6370680706908824752)
XLA Ops:
  0.0 29.0 %shard_map.73 = bf16[1,1,128,2048]{3,2,1,0:T(8,128)(2,1)S(1)} custom-call(bf16[1,128,2048]{2,1,0:T(8,128)(2,1)} %x_ref.1, s32[4,2,4]{2,1,0:T(2,128)} %bitcast.1, s32[1,16]{1,0:T(1,128)} %valid_hbm.1, f32[3]{0:T(128)} %defocus_hbm.1, f32[3]{0:T(128)} %weights_hbm.1, f32[2,128,128]{2,1,0:T(8,128)} %constant.5.clone.base_ref, bf16[256,256]{1,0:T(8,128)(2,1)} %constant.8.right_ref), custom_call_target="tpu_custom_call" | custom-call | tf_op jit(solution)/shard_map/pallas_call | solution.py:599
  29.0 0.8 %copy.9 = bf16[1,1,128,2048]{3,2,1,0:T(8,128)(2,1)} copy(bf16[1,1,128,2048]{3,2,1,0:T(8,128)(2,1)S(1)} %shard_map.73) | data formatting | bytes 1048576

commit v6 on v5

--- a/solution.py
+++ b/solution.py
@@ -14,9 +14,10 @@
 REACH = 2
 GROUP = 8
 BATCH = 4
-LEAD = 2
+LEAD = 3
 PACE = 2
-DETOUR = 1
+EARLY = 2
+DETOUR = 2
 MESH = pl.DeviceIdType.MESH
 SIN = (3.141582022082025, -5.167142794167084, 2.541899009948703, -0.5546361567315732)
 COS = (0.999999953466345, -4.934792858633932, 4.058411913339297, -1.3318801559459539, 0.21969678799073292)
@@ -76,12 +77,13 @@
     pairs = blocks // 2
     is_front, is_back = core == 0, core == 1
 
+    first, last = tile < 2, tile >= tiles - 2
+    ahead = jnp.where(first, pairs - EARLY, pairs)
+
     barrier = pltpu.get_barrier_semaphore()
 
     def greet(device):
         pl.semaphore_signal(barrier, inc=1, device_id=device, device_id_type=MESH)
-
-    first, last = tile < 2, tile >= tiles - 2
 
     @pl.when(is_back)
     def _():
@@ -370,7 +372,7 @@
                 pass_on(j)
                 return carry
 
-            lax.fori_loop(1, pairs, step, 0)
+            lax.fori_loop(1, ahead, step, 0)
 
     @pl.when(is_back)
     def _():
@@ -439,12 +441,12 @@
 
         lax.fori_loop(0, pairs, rows_step, 0)
 
-        def cols(index, g):
+        def cols(index, g, size):
             rows = []
-            for j in range(BATCH):
+            for j in range(size):
                 parts = []
                 for layer in range(2):
-                    begin = plans[index][layer][4] + 2 * (g * BATCH + j)
+                    begin = plans[index][layer][4] + 2 * (g * size + j)
                     for b in range(3):
                         parts.append(moved[layer, index, (begin + b) & (blocks - 1)])
                 rows.append(jnp.concatenate(parts, 1))
@@ -452,30 +454,34 @@
                 jnp.concatenate(rows, 0), back_slide[index], preferred_element_type=jnp.float32
             )
 
+        def send_pair(j):
+            for b in range(2):
+                across_copy(2 * j + b).start()
+
         def give_step(g, carry):
-            total = cols(0, g).astype(jnp.bfloat16)
-            for j in range(BATCH):
+            total = cols(0, g, PACE).astype(jnp.bfloat16)
+            for j in range(PACE):
                 for b in range(2):
-                    out_buf[2 * (g * BATCH + j) + b] = total[j * n : (j + 1) * n, b * n : (b + 1) * n]
+                    out_buf[2 * (g * PACE + j) + b] = total[j * n : (j + 1) * n, b * n : (b + 1) * n]
 
             @pl.when(g > 0)
             def _():
-                for k in range(2 * BATCH):
-                    across_copy(2 * (g - 1) * BATCH + k).start()
-
+                send_pair(g * PACE - 1)
+
+            for j in range(PACE - 1):
+                send_pair(g * PACE + j)
             return carry
 
-        lax.fori_loop(0, pairs // BATCH, give_step, 0)
+        lax.fori_loop(0, pairs // PACE, give_step, 0)
 
         def keep_step(g, carry):
-            total = cols(1, g)
+            total = cols(1, g, BATCH)
             for j in range(BATCH):
                 local[g * BATCH + j] = total[j * n : (j + 1) * n]
 
             @pl.when(g == 0)
             def _():
-                for k in range(2 * BATCH):
-                    across_copy(blocks - 2 * BATCH + k).start()
+                send_pair(pairs - 1)
 
             return carry
 
@@ -536,16 +542,34 @@
 
     @pl.when(passing)
     def _():
-        down_copy(blocks - 1).start()
+        @pl.when(jnp.logical_not(first))
+        def _():
+            down_copy(blocks - 1).start()
+
         await_in(0)
         field_buf[0] = field_of(0)
 
         def final_step(i, carry):
             j = 2 * i
+
+            @pl.when(j + ahead < pairs)
+            def _():
+                pass_on(j + ahead)
+
             await_in(j + 1)
             field_buf[1] = field_of(j + 1)
             spots(j, field_buf[0])
+
+            @pl.when(j + 1 + ahead < pairs)
+            def _():
+                pass_on(j + 1 + ahead)
+
             await_in(j + 2)
+
+            @pl.when((j == 0) & first)
+            def _():
+                down_copy(blocks - 1).start()
+
             field_buf[0] = field_of(j + 2)
             spots(j + 1, field_buf[1])
             return carry

time: 29.9 us -> 29.2 us (0.977)
  Pallas kernels: 29 us -> 28.3 us
    pallas_call x1, Pallas kernels: 29 us -> 28.3 us  [shards(): pl.pallas_call(functools.partial(kernel, tiles, n, blocks, slices), out_s...]
where the time goes in v6:
time: 29.2 us; the launch traced here: 29.1 us
  Pallas kernels  28.3 us (97%)
  local copies, waits for them, and re-layouts  0.8 us (3%)
    pallas_call x1, Pallas kernels, shards(): pl.pallas_call(functools.partial(kernel, tiles, n, blocks, slices), out_s...  28.3 us
    unnamed x1, local copies, waits for them, and re-layouts  0.8 us

profile of v6, /device:TPU:2, one launch (start us, length us, event | category | flops | bytes accessed | tf_op | source)
XLA Modules:
  0.0 29.1 jit_solution(2562337562967035094)
XLA Ops:
  0.0 28.3 %shard_map.73 = bf16[1,1,128,2048]{3,2,1,0:T(8,128)(2,1)S(1)} custom-call(bf16[1,128,2048]{2,1,0:T(8,128)(2,1)} %x_ref.1, s32[4,2,4]{2,1,0:T(2,128)} %bitcast.1, s32[1,16]{1,0:T(1,128)} %valid_hbm.1, f32[3]{0:T(128)} %defocus_hbm.1, f32[3]{0:T(128)} %weights_hbm.1, f32[2,128,128]{2,1,0:T(8,128)} %constant.5.clone.base_ref, bf16[256,256]{1,0:T(8,128)(2,1)} %constant.8.right_ref), custom_call_target="tpu_custom_call" | custom-call | tf_op jit(solution)/shard_map/pallas_call | solution.py:623
  28.3 0.8 %copy.9 = bf16[1,1,128,2048]{3,2,1,0:T(8,128)(2,1)} copy(bf16[1,1,128,2048]{3,2,1,0:T(8,128)(2,1)S(1)} %shard_map.73) | data formatting | bytes 1048576

commit v7 on v6

--- a/solution.py
+++ b/solution.py
@@ -16,6 +16,7 @@
 BATCH = 4
 LEAD = 3
 PACE = 2
+STRIDE = 2
 EARLY = 2
 DETOUR = 2
 MESH = pl.DeviceIdType.MESH
@@ -179,15 +180,19 @@
     twin_copy = copy(own, twin, t_send, t_recv, (tile, partner))
 
     def x_copy(j):
-        return copy(x_buf.at[j], x_in.at[j], x_send, x_recv.at[j], (mate, front))
+        return copy(x_buf.at[j], x_in.at[j], x_send, x_recv.at[lax.div(j, 2)], (mate, front))
+
+    def await_x(j):
+        part = pair_of(j)
+        copy(x_buf.at[part], x_in.at[part], x_send, x_recv.at[j], (mate, front)).wait_recv()
 
     def down_copy(j):
         return copy(out_buf.at[j], in_buf.at[j], o_send, o_recv.at[lax.div(j, 2)], (below, front))
 
     def pass_on(j):
+        await_x(j)
         for b in range(2):
             k = 2 * j + b
-            x_copy(k).wait_recv()
             out_buf[k] = (
                 tail[j, :, b * n : (b + 1) * n] + x_in[k].astype(jnp.float32)
             ).astype(jnp.bfloat16)
@@ -221,6 +226,7 @@
         )
 
     pltpu.make_async_copy(twin, own, load_sem).wait()
+    far_copy.start()
     @pl.when(odd == 0)
     def _():
         detour().start()
@@ -235,7 +241,6 @@
         for k in range(pairs):
             f_copy(k).start()
 
-    far_copy.start()
     twin_copy.start()
     for table in tables:
         table.wait()
@@ -459,20 +464,20 @@
                 across_copy(2 * j + b).start()
 
         def give_step(g, carry):
-            total = cols(0, g, PACE).astype(jnp.bfloat16)
-            for j in range(PACE):
+            total = cols(0, g, STRIDE).astype(jnp.bfloat16)
+            for j in range(STRIDE):
                 for b in range(2):
-                    out_buf[2 * (g * PACE + j) + b] = total[j * n : (j + 1) * n, b * n : (b + 1) * n]
+                    out_buf[2 * (g * STRIDE + j) + b] = total[j * n : (j + 1) * n, b * n : (b + 1) * n]
 
             @pl.when(g > 0)
             def _():
-                send_pair(g * PACE - 1)
-
-            for j in range(PACE - 1):
-                send_pair(g * PACE + j)
+                send_pair(g * STRIDE - 1)
+
+            for j in range(STRIDE - 1):
+                send_pair(g * STRIDE + j)
             return carry
 
-        lax.fori_loop(0, pairs // PACE, give_step, 0)
+        lax.fori_loop(0, pairs // STRIDE, give_step, 0)
 
         def keep_step(g, carry):
             total = cols(1, g, BATCH)
@@ -523,8 +528,8 @@
         def final_step(j, carry):
             @pl.when(is_front)
             def _():
+                await_x(j)
                 for b in range(2):
-                    x_copy(2 * j + b).wait_recv()
                     part = slice(b * n, (b + 1) * n)
                     local[j, :, part] = local[j, :, part] + x_in[2 * j + b].astype(jnp.float32)
 
@@ -656,7 +661,7 @@
                 dma, dma((6,)),
                 dma, dma((2, pairs)), dma, dma, dma((pairs,)),
                 dma, dma, dma, dma,
-                dma, dma((blocks,)), dma, dma((pairs,)), dma, dma,
+                dma, dma((pairs,)), dma, dma((pairs,)), dma, dma,
                 pltpu.SemaphoreType.REGULAR((2,)),
             ],
             compiler_params=pltpu.CompilerParams(collective_id=0, has_side_effects=True),

time: 29.2 us -> 29.3 us (level)
  no operation moved by 1% of the time
where the time goes in v7:
time: 29.3 us; the launch traced here: 29.2 us
  Pallas kernels  28.4 us (97%)
  local copies, waits for them, and re-layouts  0.8 us (3%)
    pallas_call x1, Pallas kernels, shards(): pl.pallas_call(functools.partial(kernel, tiles, n, blocks, slices), out_s...  28.4 us
    unnamed x1, local copies, waits for them, and re-layouts  0.8 us

profile of v7, /device:TPU:2, one launch (start us, length us, event | category | flops | bytes accessed | tf_op | source)
XLA Modules:
  0.0 29.2 jit_solution(12690237810237039260)
XLA Ops:
  0.0 28.4 %shard_map.73 = bf16[1,1,128,2048]{3,2,1,0:T(8,128)(2,1)S(1)} custom-call(bf16[1,128,2048]{2,1,0:T(8,128)(2,1)} %x_ref.1, s32[4,2,4]{2,1,0:T(2,128)} %bitcast.1, s32[1,16]{1,0:T(1,128)} %valid_hbm.1, f32[3]{0:T(128)} %defocus_hbm.1, f32[3]{0:T(128)} %weights_hbm.1, f32[2,128,128]{2,1,0:T(8,128)} %constant.5.clone.base_ref, bf16[256,256]{1,0:T(8,128)(2,1)} %constant.8.right_ref), custom_call_target="tpu_custom_call" | custom-call | tf_op jit(solution)/shard_map/pallas_call | solution.py:628
  28.4 0.8 %copy.9 = bf16[1,1,128,2048]{3,2,1,0:T(8,128)(2,1)} copy(bf16[1,1,128,2048]{3,2,1,0:T(8,128)(2,1)S(1)} %shard_map.73) | data formatting | bytes 1048576

commit v8 on v6

--- a/solution.py
+++ b/solution.py
@@ -13,7 +13,7 @@
 QUANT = 4
 REACH = 2
 GROUP = 8
-BATCH = 4
+BATCH = 8
 LEAD = 3
 PACE = 2
 EARLY = 2

time: 29.2 us -> 29.2 us (level)
  no operation moved by 1% of the time
where the time goes in v8:
time: 29.2 us; the launch traced here: 29.1 us
  Pallas kernels  28.3 us (97%)
  local copies, waits for them, and re-layouts  0.8 us (3%)
    pallas_call x1, Pallas kernels, shards(): pl.pallas_call(functools.partial(kernel, tiles, n, blocks, slices), out_s...  28.3 us
    unnamed x1, local copies, waits for them, and re-layouts  0.8 us

profile of v8, /device:TPU:2, one launch (start us, length us, event | category | flops | bytes accessed | tf_op | source)
XLA Modules:
  0.0 29.1 jit_solution(12898276638444834435)
XLA Ops:
  0.0 28.3 %shard_map.73 = bf16[1,1,128,2048]{3,2,1,0:T(8,128)(2,1)S(1)} custom-call(bf16[1,128,2048]{2,1,0:T(8,128)(2,1)} %x_ref.1, s32[4,2,4]{2,1,0:T(2,128)} %bitcast.1, s32[1,16]{1,0:T(1,128)} %valid_hbm.1, f32[3]{0:T(128)} %defocus_hbm.1, f32[3]{0:T(128)} %weights_hbm.1, f32[2,128,128]{2,1,0:T(8,128)} %constant.5.clone.base_ref, bf16[256,256]{1,0:T(8,128)(2,1)} %constant.8.right_ref), custom_call_target="tpu_custom_call" | custom-call | tf_op jit(solution)/shard_map/pallas_call | solution.py:623
  28.3 0.8 %copy.9 = bf16[1,1,128,2048]{3,2,1,0:T(8,128)(2,1)} copy(bf16[1,1,128,2048]{3,2,1,0:T(8,128)(2,1)S(1)} %shard_map.73) | data formatting | bytes 1048576

commit v9 on v7

--- a/solution.py
+++ b/solution.py
@@ -13,7 +13,7 @@
 QUANT = 4
 REACH = 2
 GROUP = 8
-BATCH = 4
+BATCH = 8
 LEAD = 3
 PACE = 2
 STRIDE = 2

time: 29.3 us -> 29.3 us (level)
  no operation moved by 1% of the time
where the time goes in v9:
time: 29.3 us; the launch traced here: 29.2 us
  Pallas kernels  28.3 us (97%)
  local copies, waits for them, and re-layouts  0.8 us (3%)
    pallas_call x1, Pallas kernels, shards(): pl.pallas_call(functools.partial(kernel, tiles, n, blocks, slices), out_s...  28.3 us
    unnamed x1, local copies, waits for them, and re-layouts  0.8 us

profile of v9, /device:TPU:2, one launch (start us, length us, event | category | flops | bytes accessed | tf_op | source)
XLA Modules:
  0.0 29.2 jit_solution(509821521087068557)
XLA Ops:
  0.0 28.3 %shard_map.73 = bf16[1,1,128,2048]{3,2,1,0:T(8,128)(2,1)S(1)} custom-call(bf16[1,128,2048]{2,1,0:T(8,128)(2,1)} %x_ref.1, s32[4,2,4]{2,1,0:T(2,128)} %bitcast.1, s32[1,16]{1,0:T(1,128)} %valid_hbm.1, f32[3]{0:T(128)} %defocus_hbm.1, f32[3]{0:T(128)} %weights_hbm.1, f32[2,128,128]{2,1,0:T(8,128)} %constant.5.clone.base_ref, bf16[256,256]{1,0:T(8,128)(2,1)} %constant.8.right_ref), custom_call_target="tpu_custom_call" | custom-call | tf_op jit(solution)/shard_map/pallas_call | solution.py:628
  28.4 0.8 %copy.9 = bf16[1,1,128,2048]{3,2,1,0:T(8,128)(2,1)} copy(bf16[1,1,128,2048]{3,2,1,0:T(8,128)(2,1)S(1)} %shard_map.73) | data formatting | bytes 1048576
